TPU v7x, 512 devices: a 4x2x32 block of a 4x16x32 slice. The times are simulated.
512 devices in a mesh: groups: 2 (over y), vel: 32 (over z), space: 4 (over x), spec: 2 (over core).
Axes of the slice: x: 4, y: 2, z: 32, core: 2. Of those that a mesh axis runs over, the one named last changes fastest.
The devices are a block of a 4x16x32 slice.
Arguments:
- distribution: float32 [2, 64, 64, 32768], P('spec', ('groups', 'space'), None, 'vel'), parts along dimension 1, may hold values from 0.25 to 4
- vel_order: int32 [32768], P('vel'), may hold values from 0 to 32767, each once
- species_mass: int32 [2], P('spec'), may hold values from 1 to 8
- wall_mask: int32 [64, 2], P(('groups', 'space')), parts along dimension 0, may hold values 0 or 1
- inflow_mask: int32 [64, 2], P(('groups', 'space')), parts along dimension 0, may hold values 0 or 1
Outputs:
- updated: float32 [2, 64, 64, 32768], P('spec', ('groups', 'space'), None, 'vel'), parts along dimension 1
There are 2 independent parts, one for each index of `groups`. A program takes and returns all parts, laid end to end along the dimension named above; an argument that names none is the same for every part. Nothing has to cross between parts.
Inputs may be any that keep to these rules, and one draw needn't show every extreme that they name: `vel_order`: each number from 0 to 32767 appears once.
All inputs are finite; a program needn't handle non-finite values. No bound on the sum of `wall_mask` or of `inflow_mask` on one device may be relied on, other than what follows from the above.
Results may differ from a plain program's by a relative error of at most 0.0001.
Values sent between devices are 32-bit elements; how exact they have to be, the bound alone decides.
A program may use at most 64 MiB of HBM per device.

v0:
```python
import jax
import jax.numpy as jnp
from jax import lax
from jax.sharding import PartitionSpec as P

NV = 32
NVEL = 32768


TIME_STEP = 0.1
RAREFACTION = 0.5
PORT_DENSITY = 1.0
HALF_RANGE = 4.5
PRECISE = lax.Precision.HIGHEST


def from_everyone(shard, axis):
    copies = jnp.broadcast_to(shard, (lax.axis_size(axis), *shard.shape))
    return lax.all_to_all(copies, axis, split_axis=0, concat_axis=0, tiled=True)


def of_everyone(shard, axis):
    return from_everyone(shard, axis).sum(axis=0)


def together(arrays, axis):
    vector, at, done = (jnp.concatenate([a.reshape(-1) for a in arrays]), 0, [])
    total = of_everyone(vector, axis)
    for a in arrays:
        done.append(total[at : at + a.size].reshape(a.shape))
        at += a.size
    return tuple(done)


def padded_2(cells, sides, width):
    for axis, dim in sides:
        count = lax.axis_size(axis)
        head = lax.slice_in_dim(cells, 0, width, axis=dim)
        tail = lax.slice_in_dim(cells, cells.shape[dim] - width, cells.shape[dim], axis=dim)
        cells = jnp.concatenate(
            [
                lax.ppermute(tail, axis, [(i, (i + 1) % count) for i in range(count)]),
                cells,
                lax.ppermute(head, axis, [((i + 1) % count, i) for i in range(count)]),
            ],
            axis=dim,
        )
    return cells


def lattice(lattice_ids, molecule_weight):
    spacing = 2.0 * HALF_RANGE / (NV - 1) / jnp.sqrt(molecule_weight)
    centre = (NV - 1) / 2.0
    index_a = (lattice_ids // (NV * NV)).astype(jnp.float32)
    index_b = (lattice_ids // NV % NV).astype(jnp.float32)
    index_e = (lattice_ids % NV).astype(jnp.float32)
    return (
        (index_a - centre) * spacing,
        (index_b - centre) * spacing,
        (index_e - centre) * spacing,
        spacing,
    )


def features(speed_x, speed_y, speed_z, molecule_weight):
    square = speed_x * speed_x + speed_y * speed_y + speed_z * speed_z
    unity = jnp.ones_like(speed_x)
    moment_rows = jnp.stack(
        [
            unity,
            molecule_weight * unity,
            molecule_weight * speed_x,
            molecule_weight * speed_y,
            molecule_weight * speed_z,
            0.5 * molecule_weight * square,
        ]
    )
    shape_rows = jnp.stack([unity, speed_x, speed_y, speed_z, square])
    return (moment_rows, shape_rows, square)


def wall_law(square, spacing, molecule_weight):
    return jnp.exp(
        jnp.log(NVEL * spacing**3)
        + 1.5 * jnp.log(molecule_weight / (2.0 * jnp.pi))
        - 0.5 * molecule_weight * square
    )


def wall_scale(molecule_weight):
    all_points = jnp.arange(NVEL, dtype=jnp.int32)
    speed_x, speed_y, speed_z, spacing = lattice(all_points, molecule_weight)
    square = speed_x * speed_x + speed_y * speed_y + speed_z * speed_z
    return jnp.sum(jnp.maximum(speed_y, 0.0) * wall_law(square, spacing, molecule_weight)) / NVEL


def mixture(first_moments, second_moments):
    blended_gas_sums_all = first_moments + second_moments
    count_per_volume = blended_gas_sums_all[0]
    component_weight_per_volume = blended_gas_sums_all[1]
    mean_drift_first = blended_gas_sums_all[2] / component_weight_per_volume
    mean_drift_second = blended_gas_sums_all[3] / component_weight_per_volume
    mean_drift_third = blended_gas_sums_all[4] / component_weight_per_volume
    motion_work_content = (
        mean_drift_first * mean_drift_first
        + mean_drift_second * mean_drift_second
        + mean_drift_third * mean_drift_third
    )
    cellwise_thermal_level = (
        2.0
        / 3.0
        * (blended_gas_sums_all[5] - 0.5 * component_weight_per_volume * motion_work_content)
        / count_per_volume
    )
    return (
        mean_drift_first,
        mean_drift_second,
        mean_drift_third,
        cellwise_thermal_level,
        count_per_volume / RAREFACTION,
    )


def coefficients(own_moments, blended_gas_mean, molecule_weight, spacing):
    (
        mean_drift_first,
        mean_drift_second,
        mean_drift_third,
        cellwise_thermal_level,
        collision_pace,
    ) = blended_gas_mean
    reciprocal_crowding = molecule_weight / cellwise_thermal_level
    motion_work_content = (
        mean_drift_first * mean_drift_first
        + mean_drift_second * mean_drift_second
        + mean_drift_third * mean_drift_third
    )
    leading = (
        jnp.log(own_moments[0])
        + jnp.log(NVEL * spacing**3)
        + 1.5 * jnp.log(reciprocal_crowding / (2.0 * jnp.pi))
        - 0.5 * reciprocal_crowding * motion_work_content
    )
    return jnp.stack(
        [
            leading,
            reciprocal_crowding * mean_drift_first,
            reciprocal_crowding * mean_drift_second,
            reciprocal_crowding * mean_drift_third,
            -0.5 * reciprocal_crowding,
        ]
    )


def collide(dist_rows, coeffs, collision_pace, shape_rows):
    exponent = lax.dot_general(
        coeffs,
        shape_rows,
        (((0,), (0,)), ((), ())),
        precision=PRECISE,
        preferred_element_type=jnp.float32,
    )
    return dist_rows + TIME_STEP * collision_pace[:, None] * (jnp.exp(exponent) - dist_rows)


def stream(collided, left_cells, right_cells, ghost_low, ghost_high, speed_x, speed_y):
    below_cells = jnp.concatenate([ghost_low[:, None, :], collided[:, :-1, :]], axis=1)
    above_cells = jnp.concatenate([collided[:, 1:, :], ghost_high[:, None, :]], axis=1)
    plus_x = jnp.maximum(speed_x, 0.0)
    minus_x = jnp.minimum(speed_x, 0.0)
    plus_y = jnp.maximum(speed_y, 0.0)
    minus_y = jnp.minimum(speed_y, 0.0)
    change = (
        plus_x * (collided - left_cells)
        + minus_x * (right_cells - collided)
        + plus_y * (collided - below_cells)
        + minus_y * (above_cells - collided)
    )
    return collided - TIME_STEP * change


def per_device(distribution, vel_order, species_mass, wall_mask, inflow_mask):
    local_dist = distribution[0]
    slab_rows, cross_rows, vel_count = local_dist.shape
    molecule_weight = species_mass.astype(jnp.float32)[0]
    speed_x, speed_y, speed_z, spacing = lattice(vel_order, molecule_weight)
    moment_rows, shape_rows, square = features(speed_x, speed_y, speed_z, molecule_weight)
    cell_count = slab_rows * cross_rows
    flat_dist = local_dist.reshape(cell_count, vel_count)
    partial_value = (
        lax.dot_general(
            moment_rows,
            flat_dist,
            (((1,), (1,)), ((), ())),
            precision=PRECISE,
            preferred_element_type=jnp.float32,
        )
        / NVEL
    )
    low_flux = jnp.dot(local_dist[:, 0, :], jnp.maximum(-speed_y, 0.0), precision=PRECISE) / NVEL
    high_flux = (
        jnp.dot(local_dist[:, cross_rows - 1, :], jnp.maximum(speed_y, 0.0), precision=PRECISE)
        / NVEL
    )
    wall_part = jnp.stack([low_flux, high_flux], axis=1)
    own_moments, incident = together((partial_value, wall_part), "vel")
    gathered = lax.all_gather(own_moments[None], "spec", axis=0, tiled=True)
    first_moments = gathered[0]
    second_moments = gathered[1]
    blended_gas_mean = mixture(first_moments, second_moments)
    coeffs = coefficients(own_moments, blended_gas_mean, molecule_weight, spacing)
    collision_pace = blended_gas_mean[4]
    collided = collide(flat_dist, coeffs, collision_pace, shape_rows).reshape(
        slab_rows, cross_rows, vel_count
    )
    padded = padded_2(collided, (("space", 0),), 1)
    left_cells = padded[:-2]
    right_cells = padded[2:]
    emitted = wall_law(square, spacing, molecule_weight)
    wall_weight = wall_mask.astype(jnp.float32)
    factor = (
        wall_weight * incident / wall_scale(molecule_weight)
        + inflow_mask.astype(jnp.float32) * PORT_DENSITY
    )
    ghost_low = factor[:, 0:1] * emitted[None, :]
    ghost_high = factor[:, 1:2] * emitted[None, :]
    updated = stream(collided, left_cells, right_cells, ghost_low, ghost_high, speed_x, speed_y)
    return updated[None]


def solution(mesh):
    in_specs = (
        P("spec", ("groups", "space"), None, "vel"),
        P("vel"),
        P("spec"),
        P(("groups", "space"), None),
        P(("groups", "space"), None),
    )
    out_specs = P("spec", ("groups", "space"), None, "vel")
    return jax.shard_map(
        per_device, mesh=mesh, in_specs=in_specs, out_specs=out_specs, check_vma=False
    )
```

profile of v0, /device:TPU:33, one launch (start us, length us, event | category | flops | bytes accessed | tf_op | source)
XLA Modules:
  0.0 128.4 jit_solution(3223701599492560968)
XLA Ops:
  0.0 0.0 copy-start
  0.0 0.0 copy-start.1
  0.9 0.7 broadcast_maximum_fusion
  1.6 0.7 subtract_exponential_fusion
  2.4 0.1 stack.55
  2.4 3.4 %convolution_multiply_fusion = f32[6,512]{1,0:T(8,128)S(1)} fusion(f32[6,1024]{1,0:T(8,128)S(1)} %stack.55, f32[512,1024]{1,0:T(8,128)} %bitcast.89), kind=kOutput, calls=%fused_computation.17 | convolution fusion | flops 37751808 | bytes 2134016 | tf_op jit(solution)/shard_map/dot_general | solution.py:191
  5.8 0.0 copy-done
  5.9 0.1 fusion.73
  5.9 0.1 fusion.15
  6.1 0.2 fusion.13
  6.3 0.1 copy.18
  6.4 0.1 reshape.152
  6.5 1.0 broadcast_in_dim.4
  7.4 46.3 %all-to-all-start = ((f32[32,1,3088]{2,1,0:T(1,128)}), f32[32,1,3088]{2,1,0:T(1,128)S(1)}, u32[]{:S(2)}, u32[]{:S(2)}) async-start(f32[32,1,3088]{2,1,0:T(1,128)} %broadcast_in_dim.4), calls=%async_computation | async-start | bytes 819200 | tf_op jit(solution)/shard_map/all_to_all | solution.py:19
  53.8 0.0 copy-done.1
  53.8 0.1 copy.20
  53.8 0.0 copy-done.2
  53.8 0.1 copy.21
  53.9 0.7 fusion.43
  55.2 51.8 %all-to-all-done = f32[32,1,3088]{2,1,0:T(1,128)S(1)} async-done(((f32[32,1,3088]{2,1,0:T(1,128)}), f32[32,1,3088]{2,1,0:T(1,128)S(1)}, u32[]{:S(2)}, u32[]{:S(2)}) %all-to-all-start) | async-done | bytes 395296 | tf_op jit(solution)/shard_map/all_to_all | solution.py:19
  107.0 0.2 reduce_sum.18
  107.3 3.8 %all_gather.3 = f32[2,6,512]{2,1,0:T(8,128)S(1)} all-gather(f32[1,6,512]{2,1,0:T(8,128)S(1)} %broadcast_in_dim_reshape.3), channel_id=1, replica_groups=mesh['groups'=2,'vel'=32,'space'=4,'spec'=2] {'spec'}, dimensions={0}, use_global_device_ids=true | all-gather | bytes 36864 | tf_op jit(solution)/shard_map/all_gather | solution.py:207
  111.1 0.1 reshape.155
  111.3 2.2 %multiply_add_fusion = f32[512,1024]{1,0:T(8,128)S(1)} fusion(f32[512,1024]{1,0:T(8,128)S(1)} %bitcast.91, f32[5,512]{1,0:T(8,128)S(1)} %stack.59, f32[5,1024]{1,0:T(8,128)S(1)} %stack.64, f32[512]{0:T(512)S(1)} %bitcast.102), kind=kOutput, calls=%fused_computation.16 | convolution fusion | flops 33030144 | bytes 4227072 | tf_op jit(solution)/shard_map/dot_general | solution.py:156
  113.5 3.3 %collective-permute-start = (f32[1,64,1024]{2,1,0:T(8,128)S(1)}, f32[1,64,1024]{2,1,0:T(8,128)S(1)}, u32[]{:S(2)}, u32[]{:S(2)}) collective-permute-start(f32[1,64,1024]{2,1,0:T(8,128)S(1)} %get-tuple-element.23), channel_id=1, source_target_pairs={{0,2},{2,4},{4,6},{6,0},{1,3},{3,5},{5,7},{7,1},{8,10},{10,12},{12... | collective-permute-start | bytes 786440 | tf_op jit(solution)/shard_map/ppermute | solution.py:42
  116.8 3.5 %collective-permute-start.1 = (f32[1,64,1024]{2,1,0:T(8,128)S(1)}, f32[1,64,1024]{2,1,0:T(8,128)S(1)}, u32[]{:S(2)}, u32[]{:S(2)}) collective-permute-start(f32[1,64,1024]{2,1,0:T(8,128)S(1)} %get-tuple-element.24), channel_id=1, source_target_pairs={{2,0},{4,2},{6,4},{0,6},{3,1},{5,3},{7,5},{1,7},{10,8},{12,10},{14... | collective-permute-start | bytes 786440 | tf_op jit(solution)/shard_map/ppermute | solution.py:44
  120.3 0.6 fusion.72
  120.9 0.2 slice_reduce_fusion
  121.1 0.1 broadcast_multiply_fusion
  121.2 3.4 %collective-permute-done = f32[1,64,1024]{2,1,0:T(8,128)S(1)} collective-permute-done((f32[1,64,1024]{2,1,0:T(8,128)S(1)}, f32[1,64,1024]{2,1,0:T(8,128)S(1)}, u32[]{:S(2)}, u32[]{:S(2)}) %collective-permute-start) | collective-permute-done | bytes 262176 | tf_op jit(solution)/shard_map/ppermute | solution.py:42
  124.6 1.4 %collective-permute-done.1 = f32[1,64,1024]{2,1,0:T(8,128)S(1)} collective-permute-done((f32[1,64,1024]{2,1,0:T(8,128)S(1)}, f32[1,64,1024]{2,1,0:T(8,128)S(1)}, u32[]{:S(2)}, u32[]{:S(2)}) %collective-permute-start.1) | collective-permute-done | bytes 262176 | tf_op jit(solution)/shard_map/ppermute | solution.py:44
  126.0 2.5 %fusion.7 = f32[1,8,64,1024]{3,2,1,0:T(8,128)} fusion(f32[8,64,1024]{2,1,0:T(8,128)S(1)} %bitcast.88, f32[1,64,1024]{2,1,0:T(8,128)S(1)} %collective-permute-done.1, f32[1,64,1024]{2,1,0:T(8,128)S(1)} %collective-permute-done, f32[8,63,1024]{2,1,0:T(8,128)S(1)} %get-tuple-element.22, f32[8,1,1024]{2,1,0:T(1,128)S(1)} %get-tuple-element.32, ...), kind=kLoop, calls=%fused_computation.8 | loop fusion | flops 8912896 | bytes 8929280 | tf_op jit(solution)/shard_map/broadcast_in_dim | solution.py:228
  (19 shorter events, 0.3 us)
Async XLA Ops:
  0.0 5.8 %copy-start = (f32[1,8,64,1024]{3,2,1,0:T(8,128)S(1)}, f32[1,8,64,1024]{3,2,1,0:T(8,128)}, u32[]{:S(2)}) copy-start(f32[1,8,64,1024]{3,2,1,0:T(8,128)} %param.5) | copy-start | bytes 6291460
  0.0 53.8 %copy-start.1 = (s32[8,2]{0,1:T(2,128)S(1)}, s32[8,2]{0,1:T(2,128)}, u32[]{:S(2)}) copy-start(s32[8,2]{0,1:T(2,128)} %param.8) | copy-start | bytes 196
  0.0 53.8 %copy-start.2 = (s32[8,2]{0,1:T(2,128)S(1)}, s32[8,2]{0,1:T(2,128)}, u32[]{:S(2)}) copy-start(s32[8,2]{0,1:T(2,128)} %param.9) | copy-start | bytes 196
  7.4 99.6 %all-to-all-start = ((f32[32,1,3088]{2,1,0:T(1,128)}), f32[32,1,3088]{2,1,0:T(1,128)S(1)}, u32[]{:S(2)}, u32[]{:S(2)}) async-start(f32[32,1,3088]{2,1,0:T(1,128)} %broadcast_in_dim.4), calls=%async_computation | async-start | bytes 819200 | tf_op jit(solution)/shard_map/all_to_all | solution.py:19
  113.5 11.1 %collective-permute-start = (f32[1,64,1024]{2,1,0:T(8,128)S(1)}, f32[1,64,1024]{2,1,0:T(8,128)S(1)}, u32[]{:S(2)}, u32[]{:S(2)}) collective-permute-start(f32[1,64,1024]{2,1,0:T(8,128)S(1)} %get-tuple-element.23), channel_id=1, source_target_pairs={{0,2},{2,4},{4,6},{6,0},{1,3},{3,5},{5,7},{7,1},{8,10},{10,12},{12... | collective-permute-start | bytes 786440 | tf_op jit(solution)/shard_map/ppermute | solution.py:42
  116.8 9.2 %collective-permute-start.1 = (f32[1,64,1024]{2,1,0:T(8,128)S(1)}, f32[1,64,1024]{2,1,0:T(8,128)S(1)}, u32[]{:S(2)}, u32[]{:S(2)}) collective-permute-start(f32[1,64,1024]{2,1,0:T(8,128)S(1)} %get-tuple-element.24), channel_id=1, source_target_pairs={{2,0},{4,2},{6,4},{0,6},{3,1},{5,3},{7,5},{1,7},{10,8},{12,10},{14... | collective-permute-start | bytes 786440 | tf_op jit(solution)/shard_map/ppermute | solution.py:44
where the time goes:
time: 129 us; the launch traced here: 128 us
  waiting for transfers between devices  56.5 us (44%)
  starting transfers between devices  53.1 us (41%)
  matrix products  5.9 us (5%)
  other arithmetic  5.1 us (4%)
  blocking collectives  3.77 us (3%)
  local copies, waits for them, and re-layouts  2.4 us (2%)
  between operations  1.68 us (1%)
    all_to_all x1, waiting for transfers between devices, from_everyone(): return lax.all_to_all(copies, axis, split_axis=0, concat_axis=0, tiled=True)  51.8 us
    all_to_all x1, starting transfers between devices, from_everyone(): return lax.all_to_all(copies, axis, split_axis=0, concat_axis=0, tiled=True)  46.3 us
    all_gather x1, blocking collectives, per_device(): gathered = lax.all_gather(own_moments[None], 'spec', axis=0, tiled=True)  3.77 us
    ppermute x1, starting transfers between devices, padded_2(): lax.ppermute(head, axis, [((i + 1) % count, i) for i in range(count)])  3.49 us
    dot_general x1, matrix products, per_device(): lax.dot_general(moment_rows, flat_dist, (((1,), (1,)), ((), ())), precisi...  3.39 us
    ppermute x1, waiting for transfers between devices, padded_2(): lax.ppermute(tail, axis, [(i, (i + 1) % count) for i in range(count)])  3.39 us
    ppermute x1, starting transfers between devices, padded_2(): lax.ppermute(tail, axis, [(i, (i + 1) % count) for i in range(count)])  3.29 us
  transfers between devices with their start and end apart: 3, of which 3 were waited for; matrix products, arithmetic and copies ran while one was open for 1% of the time, Pallas kernels for 0%

commit v1 on v0

v1 whole, which is shorter than its diff:
```python
import math

import jax
import jax.numpy as jnp
from jax import lax
from jax.experimental import pallas as pl
from jax.experimental.pallas import tpu as pltpu
from jax.sharding import PartitionSpec as P

NV = 32
NVEL = NV**3
BITS = NV.bit_length() - 1

TIME_STEP = 0.1
RAREFACTION = 0.5
PORT_DENSITY = 1.0
HALF_RANGE = 4.5
CENTRE = (NV - 1) / 2.0
STEP = 2.0 * HALF_RANGE / (NV - 1)
KAPPA = STEP * STEP
LOG2E = math.log2(math.e)

NEAR = 4
FAN = 4

F32 = jnp.float32
BF16 = jnp.bfloat16
MESH = pl.DeviceIdType.MESH


def pieces(rows):
    high = rows.astype(BF16).astype(F32)
    rest = rows - high
    middle = rest.astype(BF16).astype(F32)
    return jnp.concatenate([high, middle, rest - middle], axis=0).astype(BF16)


def lattice(order):
    index_a = lax.shift_right_logical(order, 2 * BITS).astype(F32)
    index_b = (lax.shift_right_logical(order, BITS) & (NV - 1)).astype(F32)
    index_e = (order & (NV - 1)).astype(F32)
    return index_a - CENTRE, index_b - CENTRE, index_e - CENTRE


def split_square(a, b, e):
    square = a * a + b * b + e * e
    coarse = jnp.floor(square * (1.0 / 32.0)) * 32.0
    return square, coarse, square - coarse


def rows_of(choices, shape):
    row = lax.broadcasted_iota(jnp.int32, shape, 0)
    out = choices[-1]
    for i in range(len(choices) - 2, -1, -1):
        out = jnp.where(row == i, choices[i], out)
    return out


def kernel(
    dist_in, order_in, mass_in, wall_in, inflow_in, out,
    order, mass, wall, inflow, msg, inbox, far_out, far_in, coef, halo_d, halo_c,
    w, lane, flux, coll,
    small_sem, msg_send, inbox_sem, far_send, far_recv, coef_send, coef_recv,
    halo_d_send, halo_d_recv, halo_c_send, halo_c_recv, ready,
):
    z, x, s = lax.axis_index("vel"), lax.axis_index("space"), lax.axis_index("spec")
    nz, nx = lax.axis_size("vel"), lax.axis_size("space")
    left, right = lax.rem(x + nx - 1, nx), lax.rem(x + 1, nx)
    d = dist_in.at[0]
    slab, cross, vel = d.shape
    pairs = slab // 2
    cells = slab * cross
    is_root = z == 0
    is_leader = lax.rem(z, FAN) == 0
    leader = z - lax.rem(z, FAN)

    def near(i):
        return (i <= NEAR) | (i >= nz - NEAR)

    barrier = pltpu.get_barrier_semaphore()

    def signal(sem, **where):
        pl.semaphore_signal(sem, inc=1, device_id=where, device_id_type=MESH)

    smalls = [
        pltpu.make_async_copy(order_in, order, small_sem.at[0]),
        pltpu.make_async_copy(mass_in, mass, small_sem.at[1]),
        pltpu.make_async_copy(wall_in, wall, small_sem.at[2]),
        pltpu.make_async_copy(inflow_in, inflow, small_sem.at[3]),
    ]
    for copy in smalls:
        copy.start()

    signal(barrier, space=left)
    signal(barrier, space=right)

    @pl.when(is_root)
    def _():
        signal(barrier, spec=1 - s)

        def tell(i, carry):
            @pl.when((s == 1) | near(i))
            def _():
                signal(barrier, vel=i, spec=0)
                signal(barrier, vel=i, spec=1)

            return carry

        lax.fori_loop(1, nz, tell, 0)

    @pl.when(is_leader & (z > 0))
    def _():
        for k in range(1, FAN):
            signal(barrier, vel=z + k)

    smalls[0].wait()
    smalls[1].wait()
    a, b, e = lattice(jnp.broadcast_to(order[...], (8, vel)))
    square, coarse, fine = split_square(a, b, e)
    phi = rows_of([jnp.ones_like(a), jnp.ones_like(a), a, b, e, coarse, fine, jnp.abs(b)], a.shape)
    phi = phi.astype(BF16)

    m = jnp.full((8, 128), mass[0], jnp.int32).astype(F32)
    root_m = jnp.sqrt(m)
    unit = jnp.full((8, 128), 1.0 / NVEL, F32)
    speed = root_m * (STEP / NVEL)
    energy = jnp.full((8, 128), 0.5 * KAPPA / NVEL, F32)
    scale = rows_of([unit, m * unit, speed, speed, speed, energy, energy, speed], m.shape)
    nt = (((1,), (1,)), ((), ()))
    for p in range(pairs):
        block = d[2 * p : 2 * p + 2].reshape(2 * cross, vel)
        high = block.astype(BF16)
        low = (block - high.astype(F32)).astype(BF16)
        part = lax.dot_general(phi, high, nt, preferred_element_type=F32)
        part += lax.dot_general(phi, low, nt, preferred_element_type=F32)
        msg[:, 128 * p : 128 * (p + 1)] = part * scale

    def one(flag):
        return jnp.where(flag, 1, 0)

    pl.semaphore_wait(
        barrier,
        2 + one(is_root) + one(z > 0) * (1 + one(near(z))) + one((z > FAN) & (leader != z)),
    )

    def to_root(core):
        slot = one(s != core)
        return pltpu.make_async_remote_copy(
            src_ref=msg,
            dst_ref=inbox.at[z, slot],
            send_sem=msg_send.at[core],
            recv_sem=inbox_sem.at[z, slot],
            device_id={"vel": 0, "spec": core},
            device_id_type=MESH,
        )

    def to_partner():
        return pltpu.make_async_remote_copy(
            src_ref=msg,
            dst_ref=inbox.at[0, 1],
            send_sem=msg_send.at[0],
            recv_sem=inbox_sem.at[0, 1],
            device_id={"spec": 1 - s},
            device_id_type=MESH,
        )

    @pl.when(z > 0)
    def _():
        to_root(1).start()

        @pl.when(near(z))
        def _():
            to_root(0).start()

    @pl.when(is_root)
    def _():
        to_partner().start()

    def halo_copy(src, box, sends, recvs, side):
        return pltpu.make_async_remote_copy(
            src_ref=src,
            dst_ref=box.at[side],
            send_sem=sends.at[side],
            recv_sem=recvs.at[side],
            device_id={"space": right if side == 0 else left},
            device_id_type=MESH,
        )

    halo_ds = [
        halo_copy(d.at[slab - 1], halo_d, halo_d_send, halo_d_recv, 0),
        halo_copy(d.at[0], halo_d, halo_d_send, halo_d_recv, 1),
    ]
    for copy in halo_ds:
        copy.start()

    @pl.when((z > FAN) & (leader != z))
    def _():
        signal(ready, vel=leader)

    speed_unit = (STEP / root_m)[:, :1]
    ones = jnp.ones((8, vel), F32)
    zeros = jnp.zeros((8, 128), F32)
    last = lax.broadcasted_iota(jnp.int32, (8, 128), 0)
    table = rows_of([ones, a, b, e, coarse, fine, 0.0 * ones, 0.0 * ones], ones.shape)
    keep = jnp.where(last == 6, 1.0, zeros)
    emit = jnp.where(last == 7, 1.0, zeros)
    table = jnp.concatenate([table, keep, emit], axis=1)
    w[...] = jnp.concatenate([table, table, table], axis=0).astype(BF16)
    go_x = TIME_STEP * speed_unit * jnp.abs(a)
    go_y = TIME_STEP * speed_unit * jnp.abs(b)
    law_unit = NVEL * (KAPPA / (2.0 * math.pi)) ** 1.5
    law = law_unit * jnp.exp(-0.5 * KAPPA * square)
    lane[...] = rows_of([1.0 - go_x - go_y, go_x, go_y, a, b, law, law, law], ones.shape)

    def coef_copy(target):
        return pltpu.make_async_remote_copy(
            src_ref=coef,
            dst_ref=coef,
            send_sem=coef_send.at[target],
            recv_sem=coef_recv,
            device_id={"vel": target},
            device_id_type=MESH,
        )

    @pl.when(is_root)
    def _():
        for copy in smalls[2:]:
            copy.wait()
        shape = (1, cells)
        spot = lax.broadcasted_iota(jnp.int32, shape, 1)
        wall_row = jnp.zeros(shape, F32)
        port_row = jnp.zeros(shape, F32)
        for i in range(slab):
            for side in range(2):
                here = spot == i * cross + side * (cross - 1)
                wall_row = jnp.where(here, jnp.full(shape, wall[side, i], jnp.int32).astype(F32), wall_row)
                port_row = jnp.where(here, jnp.full(shape, inflow[side, i], jnp.int32).astype(F32), port_row)
        mass_row = jnp.full(shape, mass[0], jnp.int32).astype(F32)
        point = lax.broadcasted_iota(jnp.int32, shape, 1)
        offset = point.astype(F32) - CENTRE
        bell = jnp.where(point < NV, jnp.exp(-0.5 * KAPPA * offset * offset), 0.0)
        bell_sum = jnp.sum(bell, axis=1, keepdims=True)
        flow_sum = jnp.sum(jnp.maximum(offset, 0.0) * bell, axis=1, keepdims=True)
        root_row = jnp.sqrt(mass_row)
        scale_row = (KAPPA / (2.0 * math.pi)) ** 1.5 * flow_sum * bell_sum * bell_sum
        wall_row = wall_row / (2.0 * STEP * root_row * scale_row)
        port_row = port_row * PORT_DENSITY
        sign = jnp.where(lax.rem(spot, cross) == 0, -1.0, 1.0)

        def arrive(i, slot):
            pltpu.make_async_remote_copy(
                src_ref=msg,
                dst_ref=inbox.at[i, slot],
                send_sem=msg_send.at[0],
                recv_sem=inbox_sem.at[i, slot],
                device_id={"spec": 1 - s},
                device_id_type=MESH,
            ).wait_recv()
            return inbox[i, slot]

        def take(i, carry):
            own, other = carry
            return own + arrive(i, 0), other + arrive(i, 1)

        def far_copy():
            return pltpu.make_async_remote_copy(
                src_ref=far_out,
                dst_ref=far_in,
                send_sem=far_send,
                recv_sem=far_recv,
                device_id={"spec": 1 - s},
                device_id_type=MESH,
            )

        if nz > 2 * NEAR + 1:

            @pl.when(s == 1)
            def _():
                nothing = jnp.zeros((8, cells), F32)
                own, other = lax.fori_loop(NEAR + 1, nz - NEAR, take, (nothing, nothing))
                far_out[0] = other
                far_out[1] = own
                far_in[0] = own
                far_in[1] = other
                far_copy().start()

            @pl.when(s == 0)
            def _():
                far_copy().wait_recv()

            sums = (far_in[0], far_in[1])
        else:
            sums = (jnp.zeros((8, cells), F32), jnp.zeros((8, cells), F32))
        sums = (sums[0] + msg[...], sums[1] + arrive(0, 1))
        nears = [i for i in range(1, nz) if i <= NEAR or i >= nz - NEAR]
        for i in nears:
            sums = take(i, sums)
        own, other = sums
        total = own + other

        density = total[0:1]
        per_density = 1.0 / density
        weight = total[1:2]
        per_weight = 1.0 / weight
        flow_x = total[2:3] * per_weight
        flow_y = total[3:4] * per_weight
        flow_z = total[4:5] * per_weight
        flow_square = flow_x * flow_x + flow_y * flow_y + flow_z * flow_z
        heat = 2.0 / 3.0 * (total[5:6] + total[6:7] - 0.5 * weight * flow_square) * per_density
        sharp = mass_row / heat
        pace = (TIME_STEP / RAREFACTION) * density
        spacing = STEP / root_row
        bulk = sharp * (1.0 / (2.0 * math.pi))
        height = own[0:1] * pace * (NVEL * spacing * spacing * spacing) * bulk * jnp.sqrt(bulk)
        coef[0:1] = LOG2E * (jnp.log(height) - 0.5 * sharp * flow_square)
        slope = LOG2E * sharp * spacing
        coef[1:2] = slope * flow_x
        coef[2:3] = slope * flow_y
        coef[3:4] = slope * flow_z
        curve = -0.5 * slope * spacing
        coef[4:5] = curve
        coef[5:6] = curve
        coef[6:7] = 1.0 - pace
        coef[7:8] = wall_row * (own[7:8] + sign * own[3:4]) + port_row

    @pl.when(is_root)
    def _():
        for k in range(1, min(FAN, nz)):
            coef_copy(k).start()

    @pl.when(jnp.logical_not(is_root))
    def _():
        coef_copy(0).wait_recv()

    halo_cs = [
        halo_copy(coef.at[:, pl.ds(cells - 128, 128)], halo_c, halo_c_send, halo_c_recv, 0),
        halo_copy(coef.at[:, pl.ds(0, 128)], halo_c, halo_c_send, halo_c_recv, 1),
    ]
    for copy in halo_cs:
        copy.start()

    @pl.when(is_root)
    def _():
        for k in range(FAN, nz, FAN):
            coef_copy(k).start()

    @pl.when(is_leader & (z > 0))
    def _():
        pl.semaphore_wait(ready, FAN - 1)
        for k in range(1, FAN):
            coef_copy(z + k).start()

    tn = (((0,), (0,)), ((), ()))
    width = 256

    def collide(parts, rows, put, put_flux):
        side = lax.dot_general(parts, w[:, vel : vel + 256], tn, preferred_element_type=F32)
        stay = jnp.concatenate([side[:, :128]] * (width // 128), axis=1)
        if put_flux is not None:
            put_flux(side[:, 128:].reshape(2, cross, 128))
        for c in range(0, vel, width):
            power = lax.dot_general(parts, w[:, c : c + width], tn, preferred_element_type=F32)
            old = rows(c).reshape(2 * cross, width)
            put(c, (old * stay + jnp.exp2(power)).reshape(2, cross, width))

    for p in range(pairs):

        def rows(c, p=p):
            return d[2 * p : 2 * p + 2, :, c : c + width]

        def put(c, value, p=p):
            coll[2 * p + 1 : 2 * p + 3, :, c : c + width] = value

        def put_flux(value, p=p):
            flux[2 * p : 2 * p + 2] = value

        collide(pieces(coef[:, 128 * p : 128 * (p + 1)]), rows, put, put_flux)

    level = lax.broadcasted_iota(jnp.int32, (cross, 128), 0)

    def stream(i):
        low_flux = flux[i, 0:1]
        high_flux = flux[i, cross - 1 : cross]
        for c in range(0, vel, 128):
            cols = slice(c, c + 128)
            here = coll[i + 1, :, cols]
            law = lane[5:6, cols]
            below = jnp.where(level == 0, low_flux * law, pltpu.roll(here, 1, 0))
            above = jnp.where(level == cross - 1, high_flux * law, pltpu.roll(here, cross - 1, 0))
            beside = jnp.where(lane[3:4, cols] > 0.0, coll[i, :, cols], coll[i + 2, :, cols])
            over = jnp.where(lane[4:5, cols] > 0.0, below, above)
            out[0, i, :, cols] = (
                lane[0:1, cols] * here + lane[1:2, cols] * beside + lane[2:3, cols] * over
            )

    for i in range(1, slab - 1):
        stream(i)

    for copy in halo_ds + halo_cs:
        copy.wait_recv()
    spot = lax.broadcasted_iota(jnp.int32, (8, 128), 1)
    beside = jnp.where(spot < cross, halo_c[1], halo_c[0])

    def rows(c):
        return jnp.concatenate([halo_d[1:2, :, c : c + width], halo_d[0:1, :, c : c + width]], 0)

    def put(c, value):
        coll[slab + 1, :, c : c + width] = value[0]
        coll[0, :, c : c + width] = value[1]

    collide(pieces(beside), rows, put, None)
    stream(0)
    stream(slab - 1)

    for copy in halo_ds + halo_cs:
        copy.wait_send()

    @pl.when(z > 0)
    def _():
        to_root(1).wait_send()
        for copy in smalls[2:]:
            copy.wait()

        @pl.when(near(z))
        def _():
            to_root(0).wait_send()

    @pl.when(is_root)
    def _():
        to_partner().wait_send()
        for k in [*range(1, min(FAN, nz)), *range(FAN, nz, FAN)]:
            coef_copy(k).wait_send()
        if nz > 2 * NEAR + 1:

            @pl.when(s == 1)
            def _():
                pltpu.make_async_remote_copy(
                    src_ref=far_out,
                    dst_ref=far_in,
                    send_sem=far_send,
                    recv_sem=far_recv,
                    device_id={"spec": 1 - s},
                    device_id_type=MESH,
                ).wait_send()

    @pl.when(is_leader & (z > 0))
    def _():
        for k in range(1, FAN):
            coef_copy(z + k).wait_send()


def per_device(distribution, vel_order, species_mass, wall_mask, inflow_mask):
    _, slab, cross, vel = distribution.shape
    nz = lax.axis_size("vel")
    cells = slab * cross
    hbm = pl.BlockSpec(memory_space=pltpu.HBM)
    dma = pltpu.SemaphoreType.DMA
    return pl.pallas_call(
        kernel,
        out_shape=jax.ShapeDtypeStruct(distribution.shape, F32),
        in_specs=[pl.BlockSpec(memory_space=pltpu.VMEM)] + [hbm] * 4,
        out_specs=pl.BlockSpec(memory_space=pltpu.VMEM),
        scratch_shapes=[
            pltpu.VMEM((1, vel), jnp.int32),
            pltpu.SMEM(species_mass.shape, jnp.int32),
            pltpu.SMEM((2, slab), jnp.int32),
            pltpu.SMEM((2, slab), jnp.int32),
            pltpu.VMEM((8, cells), F32),
            pltpu.VMEM((nz, 2, 8, cells), F32),
            pltpu.VMEM((2, 8, cells), F32),
            pltpu.VMEM((2, 8, cells), F32),
            pltpu.VMEM((8, cells), F32),
            pltpu.VMEM((2, cross, vel), F32),
            pltpu.VMEM((2, 8, 128), F32),
            pltpu.VMEM((24, vel + 256), BF16),
            pltpu.VMEM((8, vel), F32),
            pltpu.VMEM((slab, cross, 128), F32),
            pltpu.VMEM((slab + 2, cross, vel), F32),
            dma((4,)),
            dma((2,)),
            dma((nz, 2)),
            dma(()),
            dma(()),
            dma((nz,)),
            dma(()),
            dma((2,)),
            dma((2,)),
            dma((2,)),
            dma((2,)),
            pltpu.SemaphoreType.REGULAR,
        ],
        compiler_params=pltpu.CompilerParams(
            collective_id=0, has_side_effects=True, vmem_limit_bytes=32 * 1024 * 1024
        ),
    )(distribution, vel_order.reshape(1, vel), species_mass, wall_mask.T, inflow_mask.T)


def solution(mesh):
    in_specs = (
        P("spec", ("groups", "space"), None, "vel"),
        P("vel"),
        P("spec"),
        P(("groups", "space"), None),
        P(("groups", "space"), None),
    )
    out_specs = P("spec", ("groups", "space"), None, "vel")
    return jax.shard_map(
        per_device, mesh=mesh, in_specs=in_specs, out_specs=out_specs, check_vma=False
    )
```

time: 129 us -> 64 us (0.50)
  the two profiles are of different devices: /device:TPU:33 before, /device:TPU:160 now
where the time goes in v1:
time: 64 us; the launch traced here: 63.8 us
  Pallas kernels  58.2 us (91%)
  local copies, waits for them, and re-layouts  4.95 us (8%)
  between operations  0.67 us (1%)
    pallas_call x1, Pallas kernels, per_device(): pl.pallas_call(kernel, out_shape=jax.ShapeDtypeStruct(distribution.shape,...  58.2 us
    unnamed x9, local copies, waits for them, and re-layouts  4.95 us

profile of v1, /device:TPU:160, one launch (start us, length us, event | category | flops | bytes accessed | tf_op | source)
XLA Modules:
  0.0 63.8 jit_solution(7069086585195134986)
XLA Ops:
  0.7 0.0 copy-start
  0.7 1.6 %copy-done = f32[1,8,64,1024]{3,2,1,0:T(8,128)S(1)} copy-done((f32[1,8,64,1024]{3,2,1,0:T(8,128)S(1)}, f32[1,8,64,1024]{3,2,1,0:T(8,128)}, u32[]{:S(2)}) %copy-start) | copy-done | bytes 2097176
  2.2 0.0 copy-start.1
  2.2 0.7 %copy-done.1 = s32[1024]{0:T(1024)S(1)} copy-done((s32[1024]{0:T(1024)S(1)}, s32[1024]{0:T(1024)}, u32[]{:S(2)}) %copy-start.1) | copy-done | bytes 4120
  2.9 0.0 copy-start.2
  2.9 0.7 %copy-done.2 = s32[8,2]{0,1:T(2,128)S(1)} copy-done((s32[8,2]{0,1:T(2,128)S(1)}, s32[8,2]{0,1:T(2,128)}, u32[]{:S(2)}) %copy-start.2) | copy-done | bytes 88
  3.6 0.0 copy-start.3
  3.6 0.7 %copy-done.3 = s32[8,2]{0,1:T(2,128)S(1)} copy-done((s32[8,2]{0,1:T(2,128)S(1)}, s32[8,2]{0,1:T(2,128)}, u32[]{:S(2)}) %copy-start.3) | copy-done | bytes 88
  4.3 58.2 %shard_map.55 = f32[1,8,64,1024]{3,2,1,0:T(8,128)S(1)} custom-call(f32[1,8,64,1024]{3,2,1,0:T(8,128)S(1)} %copy-done, s32[1,1024]{1,0:T(1,128)S(1)} %bitcast.3, s32[1]{0:T(128)S(6)} %copy.7.mass_in, s32[2,8]{1,0:T(2,128)S(1)} %bitcast.4, s32[2,8]{1,0:T(2,128)S(1)} %bitcast.5), custom_call_target="tpu_custom_call" | custom-call | tf_op jit(solution)/shard_map/pallas_call | solution.py:458
  62.5 1.3 %copy.8 = f32[1,8,64,1024]{3,2,1,0:T(8,128)} copy(f32[1,8,64,1024]{3,2,1,0:T(8,128)S(1)} %shard_map.55) | data formatting | bytes 4194304
Async XLA Ops:
  0.7 1.6 %copy-start = (f32[1,8,64,1024]{3,2,1,0:T(8,128)S(1)}, f32[1,8,64,1024]{3,2,1,0:T(8,128)}, u32[]{:S(2)}) copy-start(f32[1,8,64,1024]{3,2,1,0:T(8,128)} %dist_in.1) | copy-start | bytes 6291460
  2.2 0.7 %copy-start.1 = (s32[1024]{0:T(1024)S(1)}, s32[1024]{0:T(1024)}, u32[]{:S(2)}) copy-start(s32[1024]{0:T(1024)} %param.6) | copy-start | bytes 12292
  2.9 0.7 %copy-start.2 = (s32[8,2]{0,1:T(2,128)S(1)}, s32[8,2]{0,1:T(2,128)}, u32[]{:S(2)}) copy-start(s32[8,2]{0,1:T(2,128)} %param.8) | copy-start | bytes 196
  3.6 0.7 %copy-start.3 = (s32[8,2]{0,1:T(2,128)S(1)}, s32[8,2]{0,1:T(2,128)}, u32[]{:S(2)}) copy-start(s32[8,2]{0,1:T(2,128)} %param.9) | copy-start | bytes 196

commit v2 on v1

v2 whole, which is shorter than its diff:
```python
import math

import jax
import jax.numpy as jnp
from jax import lax
from jax.experimental import pallas as pl
from jax.experimental.pallas import tpu as pltpu
from jax.sharding import PartitionSpec as P

NV = 32
NVEL = NV**3
BITS = NV.bit_length() - 1

TIME_STEP = 0.1
RAREFACTION = 0.5
PORT_DENSITY = 1.0
HALF_RANGE = 4.5
CENTRE = (NV - 1) / 2.0
STEP = 2.0 * HALF_RANGE / (NV - 1)
KAPPA = STEP * STEP
LOG2E = math.log2(math.e)

ROOT = 1
ROWS = 6
FAN = 4

F32 = jnp.float32
BF16 = jnp.bfloat16
MESH = pl.DeviceIdType.MESH


def pieces(rows):
    high = rows.astype(BF16).astype(F32)
    rest = rows - high
    middle = rest.astype(BF16).astype(F32)
    return jnp.concatenate([high, middle, rest - middle], axis=0).astype(BF16)


def lattice(order):
    index_a = lax.shift_right_logical(order, 2 * BITS).astype(F32)
    index_b = (lax.shift_right_logical(order, BITS) & (NV - 1)).astype(F32)
    index_e = (order & (NV - 1)).astype(F32)
    return index_a - CENTRE, index_b - CENTRE, index_e - CENTRE


def split_square(a, b, e):
    square = a * a + b * b + e * e
    coarse = jnp.floor(square * (1.0 / 32.0)) * 32.0
    return square, coarse, square - coarse


def rows_of(choices, shape):
    row = lax.broadcasted_iota(jnp.int32, shape, 0)
    out = choices[-1]
    for i in range(len(choices) - 2, -1, -1):
        out = jnp.where(row == i, choices[i], out)
    return out


def kernel(
    dist_in, order_in, mass_in, wall_in, inflow_in, out,
    d, order, mass, wall, inflow, msg, inbox, coef, coef_other, halo_d, halo_c,
    w, lane, flux, coll,
    load_sem, small_sem, msg_send, inbox_sem, coef_send, coef_recv,
    halo_d_send, halo_d_recv, halo_c_send, halo_c_recv, ready,
):
    z, x, s = lax.axis_index("vel"), lax.axis_index("space"), lax.axis_index("spec")
    nz, nx = lax.axis_size("vel"), lax.axis_size("space")
    left, right = lax.rem(x + nx - 1, nx), lax.rem(x + 1, nx)
    slab, cross, vel = d.shape
    pairs = slab // 2
    is_root = (z == 0) & (s == ROOT)
    is_leader = lax.rem(z, FAN) == 0
    leader = z - lax.rem(z, FAN)

    barrier = pltpu.get_barrier_semaphore()

    def signal(sem, **where):
        pl.semaphore_signal(sem, inc=1, device_id=where, device_id_type=MESH)

    smalls = [
        pltpu.make_async_copy(order_in, order, small_sem.at[0]),
        pltpu.make_async_copy(mass_in, mass, small_sem.at[1]),
        pltpu.make_async_copy(wall_in, wall, small_sem.at[2]),
        pltpu.make_async_copy(inflow_in, inflow, small_sem.at[3]),
    ]
    loads = [
        pltpu.make_async_copy(
            dist_in.at[0, pl.ds(2 * p, 2)], d.at[pl.ds(2 * p, 2)], load_sem.at[p]
        )
        for p in range(pairs)
    ]
    for copy in smalls[:2] + loads + smalls[2:]:
        copy.start()

    signal(barrier, space=left)
    signal(barrier, space=right)

    @pl.when(is_root)
    def _():
        signal(barrier, spec=1 - s)

        def tell(i, carry):
            signal(barrier, vel=i, spec=0)
            signal(barrier, vel=i, spec=1)
            return carry

        lax.fori_loop(1, nz, tell, 0)

    @pl.when(is_leader & (z > 0))
    def _():
        for k in range(1, FAN):
            signal(barrier, vel=z + k)

    smalls[0].wait()
    smalls[1].wait()
    a, b, e = lattice(jnp.broadcast_to(order[...], (8, vel)))
    square, coarse, fine = split_square(a, b, e)
    phi = rows_of([jnp.ones_like(a), jnp.abs(b), a, b, e, coarse, fine, fine], a.shape)
    phi = phi.astype(BF16)

    m = jnp.full((8, 128), mass[0], jnp.int32).astype(F32)
    root_m = jnp.sqrt(m)
    unit = jnp.full((8, 128), 1.0 / NVEL, F32)
    speed = root_m * (STEP / NVEL)
    energy = jnp.full((8, 128), 0.5 * KAPPA / NVEL, F32)
    scale = rows_of([unit, speed, speed, speed, speed, energy, energy, energy], m.shape)
    row = lax.broadcasted_iota(jnp.int32, (8, 128), 0)
    height = lax.broadcasted_iota(jnp.int32, (8, 128), 1) % cross
    inner = (height > 0) & (height < cross - 1)
    nt = (((1,), (1,)), ((), ()))
    for p in range(pairs):
        loads[p].wait()
        block = d[2 * p : 2 * p + 2].reshape(2 * cross, vel)
        high = block.astype(BF16)
        low = (block - high.astype(F32)).astype(BF16)
        part = lax.dot_general(phi, high, nt, preferred_element_type=F32)
        part += lax.dot_general(phi, low, nt, preferred_element_type=F32)
        part = (part + jnp.where(row == 5, pltpu.roll(part, 7, 0), 0.0)) * scale
        msg[:, p, :] = jnp.where((row == 1) & inner, m, part)[:ROWS]

    def one(flag):
        return jnp.where(flag, 1, 0)

    pl.semaphore_wait(
        barrier, 2 + one(jnp.logical_not(is_root)) + one((z > FAN) & (leader != z))
    )

    def to_root():
        return pltpu.make_async_remote_copy(
            src_ref=msg,
            dst_ref=inbox.at[z, s],
            send_sem=msg_send,
            recv_sem=inbox_sem.at[z, s],
            device_id={"vel": 0, "spec": ROOT},
            device_id_type=MESH,
        )

    @pl.when(jnp.logical_not(is_root))
    def _():
        to_root().start()

    def halo_copy(src, box, sends, recvs, side):
        return pltpu.make_async_remote_copy(
            src_ref=src,
            dst_ref=box.at[side],
            send_sem=sends.at[side],
            recv_sem=recvs.at[side],
            device_id={"space": right if side == 0 else left},
            device_id_type=MESH,
        )

    halo_ds = [
        halo_copy(d.at[slab - 1], halo_d, halo_d_send, halo_d_recv, 0),
        halo_copy(d.at[0], halo_d, halo_d_send, halo_d_recv, 1),
    ]
    for copy in halo_ds:
        copy.start()

    @pl.when((z > FAN) & (leader != z))
    def _():
        signal(ready, vel=leader)

    speed_unit = (STEP / root_m)[:, :1]
    ones = jnp.ones((8, vel), F32)
    zeros = jnp.zeros((8, 128), F32)
    table = rows_of([ones, a, b, e, coarse, fine, 0.0 * ones, 0.0 * ones], ones.shape)
    keep = jnp.where(row == 6, 1.0, zeros)
    emit = jnp.where(row == 7, 1.0, zeros)
    table = jnp.concatenate([table, keep, emit], axis=1)
    w[...] = jnp.concatenate([table, table, table], axis=0).astype(BF16)
    go_x = TIME_STEP * speed_unit * jnp.abs(a)
    go_y = TIME_STEP * speed_unit * jnp.abs(b)
    law_unit = NVEL * (KAPPA / (2.0 * math.pi)) ** 1.5
    law = law_unit * jnp.exp(-0.5 * KAPPA * square)
    lane[...] = rows_of([1.0 - go_x - go_y, go_x, go_y, a, b, law, law, law], ones.shape)

    def coef_copy(i, core, own):
        return pltpu.make_async_remote_copy(
            src_ref=coef if own else coef_other,
            dst_ref=coef,
            send_sem=coef_send.at[i, core],
            recv_sem=coef_recv,
            device_id={"vel": i, "spec": core},
            device_id_type=MESH,
        )

    def served(places):
        nearest = sorted(places, key=lambda i: min(i, nz - i))
        return [coef_copy(i, core, core == ROOT) for i in nearest for core in (ROOT, 1 - ROOT)]

    beside, leaders = range(1, min(FAN, nz)), range(FAN, nz, FAN)

    @pl.when(is_root)
    def _():
        for copy in smalls[2:]:
            copy.wait()
        shape = (pairs, 128)
        spot = lax.broadcasted_iota(jnp.int32, shape, 0) * 128
        spot = spot + lax.broadcasted_iota(jnp.int32, shape, 1)
        wall_row = jnp.zeros(shape, F32)
        port_row = jnp.zeros(shape, F32)
        for i in range(slab):
            for side in range(2):
                here = spot == i * cross + side * (cross - 1)
                wall_row = jnp.where(here, jnp.full(shape, wall[side, i], jnp.int32).astype(F32), wall_row)
                port_row = jnp.where(here, jnp.full(shape, inflow[side, i], jnp.int32).astype(F32), port_row)
        port_row = port_row * PORT_DENSITY
        offset = spot.astype(F32) - CENTRE
        bell = jnp.where(spot < NV, jnp.exp(-0.5 * KAPPA * offset * offset), 0.0)
        bell_sum = jnp.sum(jnp.sum(bell, axis=1, keepdims=True), axis=0, keepdims=True)
        flow = jnp.maximum(offset, 0.0) * bell
        flow_sum = jnp.sum(jnp.sum(flow, axis=1, keepdims=True), axis=0, keepdims=True)
        sign = jnp.where(lax.rem(spot, cross) == 0, -1.0, 1.0)
        law_scale = (2.0 * STEP) * (KAPPA / (2.0 * math.pi)) ** 1.5 * flow_sum * bell_sum * bell_sum

        def arrive(i, core):
            pltpu.make_async_remote_copy(
                src_ref=msg,
                dst_ref=inbox.at[i, core],
                send_sem=msg_send,
                recv_sem=inbox_sem.at[i, core],
                device_id={"spec": 1 - s},
                device_id_type=MESH,
            ).wait_recv()
            return inbox[i, core]

        mine, partner = msg[...], arrive(0, 1 - ROOT)
        spot_b = lax.rem(spot, cross)
        between = (spot_b > 0) & (spot_b < cross - 1)
        masses = []
        for part in (mine, partner):
            found = jnp.where(between, part[1], 0.0)
            found = jnp.max(jnp.max(found, axis=1, keepdims=True), axis=0, keepdims=True)
            masses.append(jnp.broadcast_to(found, shape))
        spacings = [STEP / jnp.sqrt(v) for v in masses]
        walls = [wall_row / (jnp.sqrt(v) * law_scale) for v in masses]
        volumes = [
            (TIME_STEP / RAREFACTION) * NVEL * v * v * v * (0.5 / math.pi) for v in spacings
        ]

        def take(i, carry):
            first, second = carry
            return first + arrive(i, ROOT), second + arrive(i, 1 - ROOT)

        own, other = lax.fori_loop(1, nz, take, (mine, partner))

        density = own[0] + other[0]
        per_density = 1.0 / density
        weight = masses[0] * own[0] + masses[1] * other[0]
        per_weight = 1.0 / weight
        flow_x = (own[2] + other[2]) * per_weight
        flow_y = (own[3] + other[3]) * per_weight
        flow_z = (own[4] + other[4]) * per_weight
        flow_square = flow_x * flow_x + flow_y * flow_y + flow_z * flow_z
        heat = 2.0 / 3.0 * (own[5] + other[5] - 0.5 * weight * flow_square) * per_density
        per_heat = 1.0 / heat
        for part, v, h, wall_v, volume, box in (
            (own, masses[0], spacings[0], walls[0], volumes[0], coef),
            (other, masses[1], spacings[1], walls[1], volumes[1], coef_other),
        ):
            sharp = v * per_heat
            top = part[0] * density * volume * sharp * jnp.sqrt(sharp * (0.5 / math.pi))
            slope = LOG2E * h * sharp
            curve = -0.5 * h * slope
            rows = [
                LOG2E * (jnp.log(top) - 0.5 * sharp * flow_square),
                slope * flow_x,
                slope * flow_y,
                slope * flow_z,
                curve,
                curve,
                1.0 - (TIME_STEP / RAREFACTION) * density,
                wall_v * (part[1] + sign * part[3]) + port_row,
            ]
            for i, values in enumerate(rows):
                box[:, i, :] = values

        coef_copy(0, 1 - ROOT, False).start()

    @pl.when(jnp.logical_not(is_root))
    def _():
        coef_copy(z, s, True).wait_recv()

    halo_cs = [
        halo_copy(coef.at[pairs - 1], halo_c, halo_c_send, halo_c_recv, 0),
        halo_copy(coef.at[0], halo_c, halo_c_send, halo_c_recv, 1),
    ]
    for copy in halo_cs:
        copy.start()

    @pl.when(is_root)
    def _():
        for copy in served(beside):
            copy.start()

    def pass_on():
        return [coef_copy(z + k, s, True) for k in range(1, FAN)]

    @pl.when(is_leader & (z > 0))
    def _():
        pl.semaphore_wait(ready, FAN - 1)
        for copy in pass_on():
            copy.start()

    tn = (((0,), (0,)), ((), ()))
    width = 256

    def collide(parts, rows, put, put_flux):
        side = lax.dot_general(parts, w[:, vel : vel + 256], tn, preferred_element_type=F32)
        stay = jnp.concatenate([side[:, :128]] * (width // 128), axis=1)
        if put_flux is not None:
            put_flux(side[:, 128:].reshape(2, cross, 128))
        for c in range(0, vel, width):
            power = lax.dot_general(parts, w[:, c : c + width], tn, preferred_element_type=F32)
            old = rows(c).reshape(2 * cross, width)
            put(c, (old * stay + jnp.exp2(power)).reshape(2, cross, width))

    for p in range(pairs):

        def rows(c, p=p):
            return d[2 * p : 2 * p + 2, :, c : c + width]

        def put(c, value, p=p):
            coll[2 * p + 1 : 2 * p + 3, :, c : c + width] = value

        def put_flux(value, p=p):
            flux[2 * p : 2 * p + 2] = value

        collide(pieces(coef[p]), rows, put, put_flux)

    @pl.when(is_root)
    def _():
        for copy in served(leaders):
            copy.start()

    level = lax.broadcasted_iota(jnp.int32, (cross, 128), 0)

    def stream(i):
        low_flux = flux[i, 0:1]
        high_flux = flux[i, cross - 1 : cross]
        for c in range(0, vel, 128):
            cols = slice(c, c + 128)
            here = coll[i + 1, :, cols]
            law = lane[5:6, cols]
            below = jnp.where(level == 0, low_flux * law, pltpu.roll(here, 1, 0))
            above = jnp.where(level == cross - 1, high_flux * law, pltpu.roll(here, cross - 1, 0))
            beside = jnp.where(lane[3:4, cols] > 0.0, coll[i, :, cols], coll[i + 2, :, cols])
            over = jnp.where(lane[4:5, cols] > 0.0, below, above)
            out[0, i, :, cols] = (
                lane[0:1, cols] * here + lane[1:2, cols] * beside + lane[2:3, cols] * over
            )

    for i in range(1, slab - 1):
        stream(i)

    for copy in halo_ds + halo_cs:
        copy.wait_recv()
    spot = lax.broadcasted_iota(jnp.int32, (8, 128), 1)
    outer = jnp.where(spot < cross, halo_c[1], halo_c[0])

    def rows(c):
        return jnp.concatenate([halo_d[1:2, :, c : c + width], halo_d[0:1, :, c : c + width]], 0)

    def put(c, value):
        coll[slab + 1, :, c : c + width] = value[0]
        coll[0, :, c : c + width] = value[1]

    collide(pieces(outer), rows, put, None)
    stream(0)
    stream(slab - 1)

    for copy in halo_ds + halo_cs:
        copy.wait_send()

    @pl.when(jnp.logical_not(is_root))
    def _():
        to_root().wait_send()
        for copy in smalls[2:]:
            copy.wait()

    @pl.when(is_root)
    def _():
        coef_copy(0, 1 - ROOT, False).wait_send()
        for copy in served(beside) + served(leaders):
            copy.wait_send()

    @pl.when(is_leader & (z > 0))
    def _():
        for copy in pass_on():
            copy.wait_send()


def per_device(distribution, vel_order, species_mass, wall_mask, inflow_mask):
    _, slab, cross, vel = distribution.shape
    nz = lax.axis_size("vel")
    pairs = slab // 2
    hbm = pl.BlockSpec(memory_space=pltpu.HBM)

    def stay(array):
        return pltpu.with_memory_space_constraint(array, pltpu.HBM)

    dma = pltpu.SemaphoreType.DMA
    return pl.pallas_call(
        kernel,
        out_shape=jax.ShapeDtypeStruct(distribution.shape, F32),
        in_specs=[hbm] * 5,
        out_specs=pl.BlockSpec(memory_space=pltpu.VMEM),
        scratch_shapes=[
            pltpu.VMEM((slab, cross, vel), F32),
            pltpu.VMEM((1, vel), jnp.int32),
            pltpu.SMEM(species_mass.shape, jnp.int32),
            pltpu.SMEM((2, slab), jnp.int32),
            pltpu.SMEM((2, slab), jnp.int32),
            pltpu.VMEM((ROWS, pairs, 128), F32),
            pltpu.VMEM((nz, 2, ROWS, pairs, 128), F32),
            pltpu.VMEM((pairs, 8, 128), F32),
            pltpu.VMEM((pairs, 8, 128), F32),
            pltpu.VMEM((2, cross, vel), F32),
            pltpu.VMEM((2, 8, 128), F32),
            pltpu.VMEM((24, vel + 256), BF16),
            pltpu.VMEM((8, vel), F32),
            pltpu.VMEM((slab, cross, 128), F32),
            pltpu.VMEM((slab + 2, cross, vel), F32),
            dma((slab // 2,)),
            dma((4,)),
            dma(()),
            dma((nz, 2)),
            dma((nz, 2)),
            dma(()),
            dma((2,)),
            dma((2,)),
            dma((2,)),
            dma((2,)),
            pltpu.SemaphoreType.REGULAR,
        ],
        compiler_params=pltpu.CompilerParams(
            collective_id=0, has_side_effects=True, vmem_limit_bytes=32 * 1024 * 1024
        ),
    )(
        stay(distribution),
        stay(vel_order.reshape(1, vel)),
        species_mass,
        stay(wall_mask.T),
        stay(inflow_mask.T),
    )


def solution(mesh):
    in_specs = (
        P("spec", ("groups", "space"), None, "vel"),
        P("vel"),
        P("spec"),
        P(("groups", "space"), None),
        P(("groups", "space"), None),
    )
    out_specs = P("spec", ("groups", "space"), None, "vel")
    return jax.shard_map(
        per_device, mesh=mesh, in_specs=in_specs, out_specs=out_specs, check_vma=False
    )
```

time: 64 us -> 58.7 us (0.917)
  the two profiles are of different devices: /device:TPU:160 before, /device:TPU:33 now
where the time goes in v2:
time: 58.7 us; the launch traced here: 57.9 us
  Pallas kernels  56 us (95%)
  local copies, waits for them, and re-layouts  1.32 us (2%)
  between operations  0.66 us (1%)
    pallas_call x1, Pallas kernels, per_device(): pl.pallas_call(kernel, out_shape=jax.ShapeDtypeStruct(distribution.shape,...  56 us
    unnamed x1, local copies, waits for them, and re-layouts  1.32 us

profile of v2, /device:TPU:33, one launch (start us, length us, event | category | flops | bytes accessed | tf_op | source)
XLA Modules:
  0.0 57.9 jit_solution(5398361764854658017)
XLA Ops:
  0.7 56.0 %shard_map.55 = f32[1,8,64,1024]{3,2,1,0:T(8,128)S(1)} custom-call(f32[1,8,64,1024]{3,2,1,0:T(8,128)} %dist_in.1, s32[1,1024]{1,0:T(1,128)} %bitcast.3, s32[1]{0:T(128)S(6)} %copy.7.mass_in, s32[2,8]{1,0:T(2,128)} %bitcast.4, s32[2,8]{1,0:T(2,128)} %bitcast.5), custom_call_target="tpu_custom_call" | custom-call | tf_op jit(solution)/shard_map/pallas_call | solution.py:424
  56.6 1.3 %copy.8 = f32[1,8,64,1024]{3,2,1,0:T(8,128)} copy(f32[1,8,64,1024]{3,2,1,0:T(8,128)S(1)} %shard_map.55) | data formatting | bytes 4194304

commit v3 on v2

--- a/solution.py
+++ b/solution.py
@@ -22,6 +22,7 @@
 
 ROOT = 1
 ROWS = 6
+DETOUR = 3
 FAN = 4
 
 F32 = jnp.float32
@@ -59,10 +60,10 @@
 
 def kernel(
     dist_in, order_in, mass_in, wall_in, inflow_in, out,
-    d, order, mass, wall, inflow, msg, inbox, coef, coef_other, halo_d, halo_c,
+    d, order, mass, wall, inflow, msg, inbox, relay, coef, coef_other, halo_d, halo_c,
     w, lane, flux, coll,
-    load_sem, small_sem, msg_send, inbox_sem, coef_send, coef_recv,
-    halo_d_send, halo_d_recv, halo_c_send, halo_c_recv, ready,
+    load_sem, small_sem, msg_send, inbox_sem, relay_sem, coef_send, coef_recv,
+    halo_d_send, halo_d_recv, halo_c_send, halo_c_recv, halo_r_send, ready,
 ):
     z, x, s = lax.axis_index("vel"), lax.axis_index("space"), lax.axis_index("spec")
     nz, nx = lax.axis_size("vel"), lax.axis_size("space")
@@ -72,6 +73,10 @@
     is_root = (z == 0) & (s == ROOT)
     is_leader = lax.rem(z, FAN) == 0
     leader = z - lax.rem(z, FAN)
+    middle = nz // 2 - 1
+    is_middle = z == middle
+    by_middle = (z > middle) & (z <= middle + DETOUR)
+    is_first = z < FAN
 
     barrier = pltpu.get_barrier_semaphore()
 
@@ -105,7 +110,18 @@
             signal(barrier, vel=i, spec=1)
             return carry
 
-        lax.fori_loop(1, nz, tell, 0)
+        lax.fori_loop(1, middle + 1, tell, 0)
+        lax.fori_loop(middle + DETOUR + 1, nz, tell, 0)
+
+    @pl.when(is_middle)
+    def _():
+        for k in range(1, DETOUR + 1):
+            signal(barrier, vel=z + k)
+
+    @pl.when(is_first)
+    def _():
+        signal(barrier, space=left, vel=0, spec=ROOT)
+        signal(barrier, space=right, vel=0, spec=ROOT)
 
     @pl.when(is_leader & (z > 0))
     def _():
@@ -134,8 +150,9 @@
         block = d[2 * p : 2 * p + 2].reshape(2 * cross, vel)
         high = block.astype(BF16)
         low = (block - high.astype(F32)).astype(BF16)
-        part = lax.dot_general(phi, high, nt, preferred_element_type=F32)
-        part += lax.dot_general(phi, low, nt, preferred_element_type=F32)
+        part = lax.dot_general(high, phi, nt, preferred_element_type=F32)
+        part += lax.dot_general(low, phi, nt, preferred_element_type=F32)
+        part = part.T
         part = (part + jnp.where(row == 5, pltpu.roll(part, 7, 0), 0.0)) * scale
         msg[:, p, :] = jnp.where((row == 1) & inner, m, part)[:ROWS]
 
@@ -143,7 +160,8 @@
         return jnp.where(flag, 1, 0)
 
     pl.semaphore_wait(
-        barrier, 2 + one(jnp.logical_not(is_root)) + one((z > FAN) & (leader != z))
+        barrier,
+        2 + one(jnp.logical_not(is_root)) + one((z > FAN) & (leader != z)) + 4 * FAN * one(is_root),
     )
 
     def to_root():
@@ -156,9 +174,23 @@
             device_id_type=MESH,
         )
 
-    @pl.when(jnp.logical_not(is_root))
+    def to_middle(i):
+        return pltpu.make_async_remote_copy(
+            src_ref=msg,
+            dst_ref=relay.at[i],
+            send_sem=msg_send,
+            recv_sem=relay_sem.at[i],
+            device_id={"vel": middle},
+            device_id_type=MESH,
+        )
+
+    @pl.when(jnp.logical_not(is_root | by_middle | is_middle))
     def _():
         to_root().start()
+
+    @pl.when(by_middle)
+    def _():
+        to_middle(z - middle - 1).start()
 
     def halo_copy(src, box, sends, recvs, side):
         return pltpu.make_async_remote_copy(
@@ -180,6 +212,15 @@
     @pl.when((z > FAN) & (leader != z))
     def _():
         signal(ready, vel=leader)
+
+    @pl.when(is_middle)
+    def _():
+        gathered = msg[...]
+        for k in range(DETOUR):
+            to_middle(k).wait_recv()
+            gathered += relay[k]
+        msg[...] = gathered
+        to_root().start()
 
     speed_unit = (STEP / root_m)[:, :1]
     ones = jnp.ones((8, vel), F32)
@@ -209,7 +250,23 @@
         nearest = sorted(places, key=lambda i: min(i, nz - i))
         return [coef_copy(i, core, core == ROOT) for i in nearest for core in (ROOT, 1 - ROOT)]
 
-    beside, leaders = range(1, min(FAN, nz)), range(FAN, nz, FAN)
+    first, others, leaders = range(1, 2), range(2, FAN), range(FAN, nz, FAN)
+
+    def borders(places):
+        return [
+            pltpu.make_async_remote_copy(
+                src_ref=(coef if core == ROOT else coef_other).at[pairs - 1 if side == 0 else 0],
+                dst_ref=halo_c.at[side],
+                send_sem=halo_r_send.at[i, core, side],
+                recv_sem=halo_c_recv.at[side],
+                device_id={"space": right if side == 0 else left, "vel": i, "spec": core},
+                device_id_type=MESH,
+            )
+            for i in places
+            for core in (ROOT, 1 - ROOT)
+            for side in range(2)
+        ]
+
 
     @pl.when(is_root)
     def _():
@@ -263,7 +320,8 @@
             first, second = carry
             return first + arrive(i, ROOT), second + arrive(i, 1 - ROOT)
 
-        own, other = lax.fori_loop(1, nz, take, (mine, partner))
+        sums = lax.fori_loop(1, middle + 1, take, (mine, partner))
+        own, other = lax.fori_loop(middle + DETOUR + 1, nz, take, sums)
 
         density = own[0] + other[0]
         per_density = 1.0 / density
@@ -297,6 +355,8 @@
                 box[:, i, :] = values
 
         coef_copy(0, 1 - ROOT, False).start()
+        for copy in borders(range(1)) + served(first) + borders(first):
+            copy.start()
 
     @pl.when(jnp.logical_not(is_root))
     def _():
@@ -306,12 +366,10 @@
         halo_copy(coef.at[pairs - 1], halo_c, halo_c_send, halo_c_recv, 0),
         halo_copy(coef.at[0], halo_c, halo_c_send, halo_c_recv, 1),
     ]
-    for copy in halo_cs:
-        copy.start()
-
-    @pl.when(is_root)
-    def _():
-        for copy in served(beside):
+
+    @pl.when(jnp.logical_not(is_first))
+    def _():
+        for copy in halo_cs:
             copy.start()
 
     def pass_on():
@@ -351,7 +409,7 @@
 
     @pl.when(is_root)
     def _():
-        for copy in served(leaders):
+        for copy in served(others) + borders(others) + served(leaders):
             copy.start()
 
     level = lax.broadcasted_iota(jnp.int32, (cross, 128), 0)
@@ -390,19 +448,31 @@
     stream(0)
     stream(slab - 1)
 
-    for copy in halo_ds + halo_cs:
+    for copy in halo_ds:
         copy.wait_send()
 
+    @pl.when(jnp.logical_not(is_first))
+    def _():
+        for copy in halo_cs:
+            copy.wait_send()
+
+    @pl.when(by_middle)
+    def _():
+        to_middle(z - middle - 1).wait_send()
+
+    @pl.when(jnp.logical_not(is_root | by_middle))
+    def _():
+        to_root().wait_send()
+
     @pl.when(jnp.logical_not(is_root))
     def _():
-        to_root().wait_send()
         for copy in smalls[2:]:
             copy.wait()
 
     @pl.when(is_root)
     def _():
         coef_copy(0, 1 - ROOT, False).wait_send()
-        for copy in served(beside) + served(leaders):
+        for copy in served([*first, *others, *leaders]) + borders(range(FAN)):
             copy.wait_send()
 
     @pl.when(is_leader & (z > 0))
@@ -434,6 +504,7 @@
             pltpu.SMEM((2, slab), jnp.int32),
             pltpu.VMEM((ROWS, pairs, 128), F32),
             pltpu.VMEM((nz, 2, ROWS, pairs, 128), F32),
+            pltpu.VMEM((DETOUR, ROWS, pairs, 128), F32),
             pltpu.VMEM((pairs, 8, 128), F32),
             pltpu.VMEM((pairs, 8, 128), F32),
             pltpu.VMEM((2, cross, vel), F32),
@@ -446,12 +517,14 @@
             dma((4,)),
             dma(()),
             dma((nz, 2)),
+            dma((DETOUR,)),
             dma((nz, 2)),
             dma(()),
             dma((2,)),
             dma((2,)),
             dma((2,)),
             dma((2,)),
+            dma((FAN, 2, 2)),
             pltpu.SemaphoreType.REGULAR,
         ],
         compiler_params=pltpu.CompilerParams(

time: 58.7 us -> 59.7 us (1.017); the launches traced: 57.9 us -> 59.6 us
  Pallas kernels: 56 us -> 57.6 us
    pallas_call x1, Pallas kernels: 56 us -> 57.6 us  [per_device(): pl.pallas_call(kernel, out_shape=jax.ShapeDtypeStruct(distribution.shape,...]
where the time goes in v3:
time: 59.7 us; the launch traced here: 59.6 us
  Pallas kernels  57.6 us (96%)
  local copies, waits for them, and re-layouts  1.32 us (2%)
  between operations  0.66 us (1%)
    pallas_call x1, Pallas kernels, per_device(): pl.pallas_call(kernel, out_shape=jax.ShapeDtypeStruct(distribution.shape,...  57.6 us
    unnamed x1, local copies, waits for them, and re-layouts  1.32 us

profile of v3, /device:TPU:33, one launch (start us, length us, event | category | flops | bytes accessed | tf_op | source)
XLA Modules:
  0.0 59.6 jit_solution(13873434380822216878)
XLA Ops:
  0.7 57.6 %shard_map.55 = f32[1,8,64,1024]{3,2,1,0:T(8,128)S(1)} custom-call(f32[1,8,64,1024]{3,2,1,0:T(8,128)} %dist_in.1, s32[1,1024]{1,0:T(1,128)} %bitcast.3, s32[1]{0:T(128)S(6)} %copy.7.mass_in, s32[2,8]{1,0:T(2,128)} %bitcast.4, s32[2,8]{1,0:T(2,128)} %bitcast.5), custom_call_target="tpu_custom_call" | custom-call | tf_op jit(solution)/shard_map/pallas_call | solution.py:494
  58.3 1.3 %copy.8 = f32[1,8,64,1024]{3,2,1,0:T(8,128)} copy(f32[1,8,64,1024]{3,2,1,0:T(8,128)S(1)} %shard_map.55) | data formatting | bytes 4194304

commit v4 on v2

--- a/solution.py
+++ b/solution.py
@@ -22,6 +22,7 @@
 
 ROOT = 1
 ROWS = 6
+LOADS = 8
 FAN = 4
 
 F32 = jnp.float32
@@ -61,8 +62,8 @@
     dist_in, order_in, mass_in, wall_in, inflow_in, out,
     d, order, mass, wall, inflow, msg, inbox, coef, coef_other, halo_d, halo_c,
     w, lane, flux, coll,
-    load_sem, small_sem, msg_send, inbox_sem, coef_send, coef_recv,
-    halo_d_send, halo_d_recv, halo_c_send, halo_c_recv, ready,
+    load_sem, small_sem, msg_send, inbox_sem, coef_send, coef_recv, pass_send,
+    halo_d_send, halo_d_recv, halo_c_send, halo_c_recv, halo_r_send, ready,
 ):
     z, x, s = lax.axis_index("vel"), lax.axis_index("space"), lax.axis_index("spec")
     nz, nx = lax.axis_size("vel"), lax.axis_size("space")
@@ -72,11 +73,16 @@
     is_root = (z == 0) & (s == ROOT)
     is_leader = lax.rem(z, FAN) == 0
     leader = z - lax.rem(z, FAN)
+    middle = nz // 2 - 1
+    is_first = z < FAN
 
     barrier = pltpu.get_barrier_semaphore()
 
     def signal(sem, **where):
         pl.semaphore_signal(sem, inc=1, device_id=where, device_id_type=MESH)
+
+    def settle(ref, sem):
+        pltpu.make_async_copy(ref, ref, sem).wait()
 
     smalls = [
         pltpu.make_async_copy(order_in, order, small_sem.at[0]),
@@ -86,9 +92,9 @@
     ]
     loads = [
         pltpu.make_async_copy(
-            dist_in.at[0, pl.ds(2 * p, 2)], d.at[pl.ds(2 * p, 2)], load_sem.at[p]
+            dist_in.at[0, pl.ds(i, slab // LOADS)], d.at[pl.ds(i, slab // LOADS)], load_sem
         )
-        for p in range(pairs)
+        for i in range(0, slab, slab // LOADS)
     ]
     for copy in smalls[:2] + loads + smalls[2:]:
         copy.start()
@@ -106,6 +112,11 @@
             return carry
 
         lax.fori_loop(1, nz, tell, 0)
+
+    @pl.when(is_first)
+    def _():
+        signal(barrier, space=left, vel=0, spec=ROOT)
+        signal(barrier, space=right, vel=0, spec=ROOT)
 
     @pl.when(is_leader & (z > 0))
     def _():
@@ -129,8 +140,8 @@
     height = lax.broadcasted_iota(jnp.int32, (8, 128), 1) % cross
     inner = (height > 0) & (height < cross - 1)
     nt = (((1,), (1,)), ((), ()))
+    settle(d, load_sem)
     for p in range(pairs):
-        loads[p].wait()
         block = d[2 * p : 2 * p + 2].reshape(2 * cross, vel)
         high = block.astype(BF16)
         low = (block - high.astype(F32)).astype(BF16)
@@ -143,7 +154,8 @@
         return jnp.where(flag, 1, 0)
 
     pl.semaphore_wait(
-        barrier, 2 + one(jnp.logical_not(is_root)) + one((z > FAN) & (leader != z))
+        barrier,
+        2 + one(jnp.logical_not(is_root)) + one((z > FAN) & (leader != z)) + 4 * FAN * one(is_root),
     )
 
     def to_root():
@@ -151,7 +163,7 @@
             src_ref=msg,
             dst_ref=inbox.at[z, s],
             send_sem=msg_send,
-            recv_sem=inbox_sem.at[z, s],
+            recv_sem=inbox_sem.at[one(z > 0) + one(z > middle)],
             device_id={"vel": 0, "spec": ROOT},
             device_id_type=MESH,
         )
@@ -164,8 +176,8 @@
         return pltpu.make_async_remote_copy(
             src_ref=src,
             dst_ref=box.at[side],
-            send_sem=sends.at[side],
-            recv_sem=recvs.at[side],
+            send_sem=sends,
+            recv_sem=recvs,
             device_id={"space": right if side == 0 else left},
             device_id_type=MESH,
         )
@@ -195,21 +207,37 @@
     law = law_unit * jnp.exp(-0.5 * KAPPA * square)
     lane[...] = rows_of([1.0 - go_x - go_y, go_x, go_y, a, b, law, law, law], ones.shape)
 
-    def coef_copy(i, core, own):
+    def coef_copy(i, core, own, sem):
         return pltpu.make_async_remote_copy(
             src_ref=coef if own else coef_other,
             dst_ref=coef,
-            send_sem=coef_send.at[i, core],
+            send_sem=sem,
             recv_sem=coef_recv,
             device_id={"vel": i, "spec": core},
             device_id_type=MESH,
         )
 
-    def served(places):
+    def served(places, sem):
         nearest = sorted(places, key=lambda i: min(i, nz - i))
-        return [coef_copy(i, core, core == ROOT) for i in nearest for core in (ROOT, 1 - ROOT)]
-
-    beside, leaders = range(1, min(FAN, nz)), range(FAN, nz, FAN)
+        return [coef_copy(i, core, core == ROOT, sem) for i in nearest for core in (ROOT, 1 - ROOT)]
+
+    first, others, leaders = range(1, 2), range(2, FAN), range(FAN, nz, FAN)
+
+    def borders(places):
+        return [
+            pltpu.make_async_remote_copy(
+                src_ref=(coef if core == ROOT else coef_other).at[pairs - 1 if side == 0 else 0],
+                dst_ref=halo_c.at[side],
+                send_sem=halo_r_send,
+                recv_sem=halo_c_recv,
+                device_id={"space": right if side == 0 else left, "vel": i, "spec": core},
+                device_id_type=MESH,
+            )
+            for i in places
+            for core in (ROOT, 1 - ROOT)
+            for side in range(2)
+        ]
+
 
     @pl.when(is_root)
     def _():
@@ -234,18 +262,8 @@
         sign = jnp.where(lax.rem(spot, cross) == 0, -1.0, 1.0)
         law_scale = (2.0 * STEP) * (KAPPA / (2.0 * math.pi)) ** 1.5 * flow_sum * bell_sum * bell_sum
 
-        def arrive(i, core):
-            pltpu.make_async_remote_copy(
-                src_ref=msg,
-                dst_ref=inbox.at[i, core],
-                send_sem=msg_send,
-                recv_sem=inbox_sem.at[i, core],
-                device_id={"spec": 1 - s},
-                device_id_type=MESH,
-            ).wait_recv()
-            return inbox[i, core]
-
-        mine, partner = msg[...], arrive(0, 1 - ROOT)
+        settle(inbox.at[0, 1 - ROOT], inbox_sem.at[0])
+        mine, partner = msg[...], inbox[0, 1 - ROOT]
         spot_b = lax.rem(spot, cross)
         between = (spot_b > 0) & (spot_b < cross - 1)
         masses = []
@@ -259,11 +277,12 @@
             (TIME_STEP / RAREFACTION) * NVEL * v * v * v * (0.5 / math.pi) for v in spacings
         ]
 
-        def take(i, carry):
-            first, second = carry
-            return first + arrive(i, ROOT), second + arrive(i, 1 - ROOT)
-
-        own, other = lax.fori_loop(1, nz, take, (mine, partner))
+        own, other = mine, partner
+        for part, (low, high) in enumerate([(1, middle + 1), (middle + 1, nz)]):
+            settle(inbox.at[pl.ds(low, high - low)], inbox_sem.at[part + 1])
+            for i in range(low, high):
+                own += inbox[i, ROOT]
+                other += inbox[i, 1 - ROOT]
 
         density = own[0] + other[0]
         per_density = 1.0 / density
@@ -296,26 +315,26 @@
             for i, values in enumerate(rows):
                 box[:, i, :] = values
 
-        coef_copy(0, 1 - ROOT, False).start()
+        coef_copy(0, 1 - ROOT, False, coef_send.at[0]).start()
+        for copy in borders(range(1)) + served(first, coef_send.at[1]) + borders(first):
+            copy.start()
 
     @pl.when(jnp.logical_not(is_root))
     def _():
-        coef_copy(z, s, True).wait_recv()
+        settle(coef, coef_recv)
 
     halo_cs = [
         halo_copy(coef.at[pairs - 1], halo_c, halo_c_send, halo_c_recv, 0),
         halo_copy(coef.at[0], halo_c, halo_c_send, halo_c_recv, 1),
     ]
-    for copy in halo_cs:
-        copy.start()
-
-    @pl.when(is_root)
-    def _():
-        for copy in served(beside):
+
+    @pl.when(jnp.logical_not(is_first))
+    def _():
+        for copy in halo_cs:
             copy.start()
 
     def pass_on():
-        return [coef_copy(z + k, s, True) for k in range(1, FAN)]
+        return [coef_copy(z + k, s, True, pass_send.at[k - 1]) for k in range(1, FAN)]
 
     @pl.when(is_leader & (z > 0))
     def _():
@@ -351,7 +370,8 @@
 
     @pl.when(is_root)
     def _():
-        for copy in served(leaders):
+        beyond = served(leaders, coef_send.at[2])
+        for copy in served(others, coef_send.at[1]) + borders(others) + beyond:
             copy.start()
 
     level = lax.broadcasted_iota(jnp.int32, (cross, 128), 0)
@@ -374,8 +394,8 @@
     for i in range(1, slab - 1):
         stream(i)
 
-    for copy in halo_ds + halo_cs:
-        copy.wait_recv()
+    settle(halo_d, halo_d_recv)
+    settle(halo_c, halo_c_recv)
     spot = lax.broadcasted_iota(jnp.int32, (8, 128), 1)
     outer = jnp.where(spot < cross, halo_c[1], halo_c[0])
 
@@ -390,20 +410,24 @@
     stream(0)
     stream(slab - 1)
 
-    for copy in halo_ds + halo_cs:
-        copy.wait_send()
+    settle(halo_d, halo_d_send)
+
+    @pl.when(jnp.logical_not(is_first))
+    def _():
+        settle(halo_c, halo_c_send)
 
     @pl.when(jnp.logical_not(is_root))
     def _():
-        to_root().wait_send()
+        settle(msg, msg_send)
         for copy in smalls[2:]:
             copy.wait()
 
     @pl.when(is_root)
     def _():
-        coef_copy(0, 1 - ROOT, False).wait_send()
-        for copy in served(beside) + served(leaders):
-            copy.wait_send()
+        settle(coef, coef_send.at[0])
+        settle(d.at[0, pl.ds(0, 8 * (FAN - 1))], coef_send.at[1])
+        settle(d.at[0, pl.ds(0, 8 * len(leaders))], coef_send.at[2])
+        settle(d.at[0, pl.ds(0, 4 * FAN)], halo_r_send)
 
     @pl.when(is_leader & (z > 0))
     def _():
@@ -442,16 +466,18 @@
             pltpu.VMEM((8, vel), F32),
             pltpu.VMEM((slab, cross, 128), F32),
             pltpu.VMEM((slab + 2, cross, vel), F32),
-            dma((slab // 2,)),
+            dma(()),
             dma((4,)),
             dma(()),
-            dma((nz, 2)),
-            dma((nz, 2)),
-            dma(()),
-            dma((2,)),
-            dma((2,)),
-            dma((2,)),
-            dma((2,)),
+            dma((3,)),
+            dma((3,)),
+            dma(()),
+            dma((FAN - 1,)),
+            dma(()),
+            dma(()),
+            dma(()),
+            dma(()),
+            dma(()),
             pltpu.SemaphoreType.REGULAR,
         ],
         compiler_params=pltpu.CompilerParams(

time: 58.7 us -> 57 us (0.971); the launches traced: 57.9 us -> 56.9 us
  Pallas kernels: 56 us -> 54.9 us
    pallas_call x1, Pallas kernels: 56 us -> 54.9 us  [per_device(): pl.pallas_call(kernel, out_shape=jax.ShapeDtypeStruct(distribution.shape,...]
where the time goes in v4:
time: 57 us; the launch traced here: 56.9 us
  Pallas kernels  54.9 us (96%)
  local copies, waits for them, and re-layouts  1.32 us (2%)
  between operations  0.66 us (1%)
    pallas_call x1, Pallas kernels, per_device(): pl.pallas_call(kernel, out_shape=jax.ShapeDtypeStruct(distribution.shape,...  54.9 us
    unnamed x1, local copies, waits for them, and re-layouts  1.32 us

profile of v4, /device:TPU:33, one launch (start us, length us, event | category | flops | bytes accessed | tf_op | source)
XLA Modules:
  0.0 56.9 jit_solution(7947138955177066499)
XLA Ops:
  0.7 54.9 %shard_map.55 = f32[1,8,64,1024]{3,2,1,0:T(8,128)S(1)} custom-call(f32[1,8,64,1024]{3,2,1,0:T(8,128)} %dist_in.1, s32[1,1024]{1,0:T(1,128)} %bitcast.3, s32[1]{0:T(128)S(6)} %copy.7.mass_in, s32[2,8]{1,0:T(2,128)} %bitcast.4, s32[2,8]{1,0:T(2,128)} %bitcast.5), custom_call_target="tpu_custom_call" | custom-call | tf_op jit(solution)/shard_map/pallas_call | solution.py:448
  55.6 1.3 %copy.8 = f32[1,8,64,1024]{3,2,1,0:T(8,128)} copy(f32[1,8,64,1024]{3,2,1,0:T(8,128)S(1)} %shard_map.55) | data formatting | bytes 4194304

commit v5 on v4

--- a/solution.py
+++ b/solution.py
@@ -59,9 +59,9 @@
 
 
 def kernel(
-    dist_in, order_in, mass_in, wall_in, inflow_in, out,
+    dist_in, order_in, mass_in, wall_in, inflow_in, coll, inner, lane, flux,
     d, order, mass, wall, inflow, msg, inbox, coef, coef_other, halo_d, halo_c,
-    w, lane, flux, coll,
+    w,
     load_sem, small_sem, msg_send, inbox_sem, coef_send, coef_recv, pass_send,
     halo_d_send, halo_d_recv, halo_c_send, halo_c_recv, halo_r_send, ready,
 ):
@@ -74,6 +74,13 @@
     is_leader = lax.rem(z, FAN) == 0
     leader = z - lax.rem(z, FAN)
     middle = nz // 2 - 1
+    rising = z <= nz // 2
+    following = jnp.where(rising, z + FAN, z - FAN)
+    preceding = jnp.where(rising, z - FAN, z + FAN)
+    passes = is_leader & (z > 0)
+    hands_on = passes & jnp.where(rising, following <= nz // 2, following > nz // 2)
+    is_handed = passes & (z != FAN) & (z != nz - FAN)
+    is_member = (z > FAN) & (leader != z)
     is_first = z < FAN
 
     barrier = pltpu.get_barrier_semaphore()
@@ -118,10 +125,14 @@
         signal(barrier, space=left, vel=0, spec=ROOT)
         signal(barrier, space=right, vel=0, spec=ROOT)
 
-    @pl.when(is_leader & (z > 0))
+    @pl.when(passes)
     def _():
         for k in range(1, FAN):
             signal(barrier, vel=z + k)
+
+    @pl.when(hands_on)
+    def _():
+        signal(barrier, vel=following)
 
     smalls[0].wait()
     smalls[1].wait()
@@ -138,7 +149,7 @@
     scale = rows_of([unit, speed, speed, speed, speed, energy, energy, energy], m.shape)
     row = lax.broadcasted_iota(jnp.int32, (8, 128), 0)
     height = lax.broadcasted_iota(jnp.int32, (8, 128), 1) % cross
-    inner = (height > 0) & (height < cross - 1)
+    amid = (height > 0) & (height < cross - 1)
     nt = (((1,), (1,)), ((), ()))
     settle(d, load_sem)
     for p in range(pairs):
@@ -148,14 +159,14 @@
         part = lax.dot_general(phi, high, nt, preferred_element_type=F32)
         part += lax.dot_general(phi, low, nt, preferred_element_type=F32)
         part = (part + jnp.where(row == 5, pltpu.roll(part, 7, 0), 0.0)) * scale
-        msg[:, p, :] = jnp.where((row == 1) & inner, m, part)[:ROWS]
+        msg[:, p, :] = jnp.where((row == 1) & amid, m, part)[:ROWS]
 
     def one(flag):
         return jnp.where(flag, 1, 0)
 
     pl.semaphore_wait(
         barrier,
-        2 + one(jnp.logical_not(is_root)) + one((z > FAN) & (leader != z)) + 4 * FAN * one(is_root),
+        2 + one(jnp.logical_not(is_root)) + one(is_member | is_handed) + 4 * FAN * one(is_root),
     )
 
     def to_root():
@@ -189,9 +200,9 @@
     for copy in halo_ds:
         copy.start()
 
-    @pl.when((z > FAN) & (leader != z))
-    def _():
-        signal(ready, vel=leader)
+    @pl.when(is_member | is_handed)
+    def _():
+        signal(ready, vel=jnp.where(is_handed, preceding, leader))
 
     speed_unit = (STEP / root_m)[:, :1]
     ones = jnp.ones((8, vel), F32)
@@ -221,7 +232,7 @@
         nearest = sorted(places, key=lambda i: min(i, nz - i))
         return [coef_copy(i, core, core == ROOT, sem) for i in nearest for core in (ROOT, 1 - ROOT)]
 
-    first, others, leaders = range(1, 2), range(2, FAN), range(FAN, nz, FAN)
+    first, others, leaders = range(1, 2), range(2, FAN), sorted({FAN, nz - FAN})
 
     def borders(places):
         return [
@@ -336,11 +347,18 @@
     def pass_on():
         return [coef_copy(z + k, s, True, pass_send.at[k - 1]) for k in range(1, FAN)]
 
-    @pl.when(is_leader & (z > 0))
-    def _():
-        pl.semaphore_wait(ready, FAN - 1)
+    def hand_on():
+        return coef_copy(following, s, True, pass_send.at[FAN - 1])
+
+    @pl.when(passes)
+    def _():
+        pl.semaphore_wait(ready, FAN - 1 + one(hands_on))
         for copy in pass_on():
             copy.start()
+
+    @pl.when(hands_on)
+    def _():
+        hand_on().start()
 
     tn = (((0,), (0,)), ((), ()))
     width = 256
@@ -374,25 +392,8 @@
         for copy in served(others, coef_send.at[1]) + borders(others) + beyond:
             copy.start()
 
-    level = lax.broadcasted_iota(jnp.int32, (cross, 128), 0)
-
-    def stream(i):
-        low_flux = flux[i, 0:1]
-        high_flux = flux[i, cross - 1 : cross]
-        for c in range(0, vel, 128):
-            cols = slice(c, c + 128)
-            here = coll[i + 1, :, cols]
-            law = lane[5:6, cols]
-            below = jnp.where(level == 0, low_flux * law, pltpu.roll(here, 1, 0))
-            above = jnp.where(level == cross - 1, high_flux * law, pltpu.roll(here, cross - 1, 0))
-            beside = jnp.where(lane[3:4, cols] > 0.0, coll[i, :, cols], coll[i + 2, :, cols])
-            over = jnp.where(lane[4:5, cols] > 0.0, below, above)
-            out[0, i, :, cols] = (
-                lane[0:1, cols] * here + lane[1:2, cols] * beside + lane[2:3, cols] * over
-            )
-
     for i in range(1, slab - 1):
-        stream(i)
+        stream(coll, lane, flux, i, inner.at[i - 1])
 
     settle(halo_d, halo_d_recv)
     settle(halo_c, halo_c_recv)
@@ -407,8 +408,6 @@
         coll[0, :, c : c + width] = value[1]
 
     collide(pieces(outer), rows, put, None)
-    stream(0)
-    stream(slab - 1)
 
     settle(halo_d, halo_d_send)
 
@@ -429,10 +428,42 @@
         settle(d.at[0, pl.ds(0, 8 * len(leaders))], coef_send.at[2])
         settle(d.at[0, pl.ds(0, 4 * FAN)], halo_r_send)
 
-    @pl.when(is_leader & (z > 0))
+    @pl.when(passes)
     def _():
         for copy in pass_on():
             copy.wait_send()
+
+    @pl.when(hands_on)
+    def _():
+        hand_on().wait_send()
+
+
+def stream(coll, lane, flux, i, out):
+    _, cross, vel = coll.shape
+    level = lax.broadcasted_iota(jnp.int32, (cross, 128), 0)
+    low_flux = flux[i, 0:1]
+    high_flux = flux[i, cross - 1 : cross]
+    for c in range(0, vel, 128):
+        cols = slice(c, c + 128)
+        here = coll[i + 1, :, cols]
+        law = lane[5:6, cols]
+        below = jnp.where(level == 0, low_flux * law, pltpu.roll(here, 1, 0))
+        above = jnp.where(level == cross - 1, high_flux * law, pltpu.roll(here, cross - 1, 0))
+        beside = jnp.where(lane[3:4, cols] > 0.0, coll[i, :, cols], coll[i + 2, :, cols])
+        over = jnp.where(lane[4:5, cols] > 0.0, below, above)
+        out[:, cols] = lane[0:1, cols] * here + lane[1:2, cols] * beside + lane[2:3, cols] * over
+
+
+def finish(coll, inner, lane, flux, out, edge, sem):
+    slab = flux.shape[0]
+    copies = [pltpu.make_async_copy(inner, out.at[0, pl.ds(1, slab - 2)], sem.at[2])]
+    copies[0].start()
+    for k, i in enumerate((0, slab - 1)):
+        stream(coll, lane, flux, i, edge.at[k])
+        copies.append(pltpu.make_async_copy(edge.at[k], out.at[0, i], sem.at[k]))
+        copies[-1].start()
+    for copy in copies:
+        copy.wait()
 
 
 def per_device(distribution, vel_order, species_mass, wall_mask, inflow_mask):
@@ -445,11 +476,21 @@
         return pltpu.with_memory_space_constraint(array, pltpu.HBM)
 
     dma = pltpu.SemaphoreType.DMA
-    return pl.pallas_call(
+    vmem = pl.BlockSpec(memory_space=pltpu.VMEM)
+    passed = [
+        jax.ShapeDtypeStruct(shape, F32)
+        for shape in [
+            (slab + 2, cross, vel),
+            (slab - 2, cross, vel),
+            (8, vel),
+            (slab, cross, 128),
+        ]
+    ]
+    parts = pl.pallas_call(
         kernel,
-        out_shape=jax.ShapeDtypeStruct(distribution.shape, F32),
+        out_shape=passed,
         in_specs=[hbm] * 5,
-        out_specs=pl.BlockSpec(memory_space=pltpu.VMEM),
+        out_specs=[vmem] * 4,
         scratch_shapes=[
             pltpu.VMEM((slab, cross, vel), F32),
             pltpu.VMEM((1, vel), jnp.int32),
@@ -463,16 +504,13 @@
             pltpu.VMEM((2, cross, vel), F32),
             pltpu.VMEM((2, 8, 128), F32),
             pltpu.VMEM((24, vel + 256), BF16),
-            pltpu.VMEM((8, vel), F32),
-            pltpu.VMEM((slab, cross, 128), F32),
-            pltpu.VMEM((slab + 2, cross, vel), F32),
             dma(()),
             dma((4,)),
             dma(()),
             dma((3,)),
             dma((3,)),
             dma(()),
-            dma((FAN - 1,)),
+            dma((FAN,)),
             dma(()),
             dma(()),
             dma(()),
@@ -490,6 +528,14 @@
         stay(wall_mask.T),
         stay(inflow_mask.T),
     )
+    return pl.pallas_call(
+        finish,
+        out_shape=jax.ShapeDtypeStruct(distribution.shape, F32),
+        in_specs=[vmem] * 4,
+        out_specs=hbm,
+        scratch_shapes=[pltpu.VMEM((2, cross, vel), F32), dma((3,))],
+        compiler_params=pltpu.CompilerParams(vmem_limit_bytes=16 * 1024 * 1024),
+    )(*parts)
 
 
 def solution(mesh):

time: 57 us -> 57.4 us (level)
  Pallas kernels: 54.9 us -> 56.6 us
  local copies, waits for them, and re-layouts: 1.32 us -> 0 us
    pallas_call x1 -> x2, Pallas kernels: 54.9 us -> 56.6 us  [the longest x1 55.3 us: per_device(): pl.pallas_call(kernel, out_shape=passed, in_specs=[hbm] * 5, out_specs=[v...]
    unnamed x1 -> x0, local copies, waits for them, and re-layouts: 1.32 us -> none
where the time goes in v5:
time: 57.4 us; the launch traced here: 57.3 us
  Pallas kernels  56.6 us (99%)
  between operations  0.66 us (1%)
    pallas_call x1, Pallas kernels, per_device(): pl.pallas_call(kernel, out_shape=passed, in_specs=[hbm] * 5, out_specs=[v...  55.3 us
    pallas_call x1, Pallas kernels, per_device(): pl.pallas_call(finish, out_shape=jax.ShapeDtypeStruct(distribution.shape,...  1.34 us

profile of v5, /device:TPU:33, one launch (start us, length us, event | category | flops | bytes accessed | tf_op | source)
XLA Modules:
  0.0 57.3 jit_solution(3584218842813447489)
XLA Ops:
  0.7 55.3 %shard_map.55 = (f32[10,64,1024]{2,1,0:T(8,128)S(1)}, f32[6,64,1024]{2,1,0:T(8,128)S(1)}, f32[8,1024]{1,0:T(8,128)S(1)}, f32[8,64,128]{2,1,0:T(8,128)S(1)}) custom-call(f32[1,8,64,1024]{3,2,1,0:T(8,128)} %dist_in.1, s32[1,1024]{1,0:T(1,128)} %bitcast.3, s32[1]{0:T(128)S(6)} %copy.6.mass_in, s32[2,8]{1,0:T(2,128)} %bitcast.4, s32[2,8]{1,0:T(2,128)} %bitcast.5), custom_call_target="tpu_custom_call" | custom-call | tf_op jit(solution)/shard_map/pallas_call | solution.py:489
  56.0 1.3 %shard_map.56 = f32[1,8,64,1024]{3,2,1,0:T(8,128)} custom-call(f32[10,64,1024]{2,1,0:T(8,128)S(1)} %get-tuple-element.9.coll, f32[6,64,1024]{2,1,0:T(8,128)S(1)} %get-tuple-element.10.inner, f32[8,1024]{1,0:T(8,128)S(1)} %get-tuple-element.11.lane, f32[8,64,128]{2,1,0:T(8,128)S(1)} %get-tuple-element.12.flux), custom_call_target="tpu_custom_call" | custom-call | tf_op jit(solution)/shard_map/pallas_call | solution.py:531

commit v6 on v5

--- a/solution.py
+++ b/solution.py
@@ -22,6 +22,7 @@
 
 ROOT = 1
 ROWS = 6
+SINGLE = 4
 LOADS = 8
 FAN = 4
 
@@ -60,9 +61,9 @@
 
 def kernel(
     dist_in, order_in, mass_in, wall_in, inflow_in, coll, inner, lane, flux,
-    d, order, mass, wall, inflow, msg, inbox, coef, coef_other, halo_d, halo_c,
+    d, order, mass, wall, inflow, msg, inbox, relay, coef, coef_other, halo_d, halo_c,
     w,
-    load_sem, small_sem, msg_send, inbox_sem, coef_send, coef_recv, pass_send,
+    load_sem, small_sem, msg_send, inbox_sem, relay_sem, coef_send, coef_recv, pass_send,
     halo_d_send, halo_d_recv, halo_c_send, halo_c_recv, halo_r_send, ready,
 ):
     z, x, s = lax.axis_index("vel"), lax.axis_index("space"), lax.axis_index("spec")
@@ -74,6 +75,13 @@
     is_leader = lax.rem(z, FAN) == 0
     leader = z - lax.rem(z, FAN)
     middle = nz // 2 - 1
+    couples = (nz - SINGLE - middle - 1) // 2
+    singles = middle + 1 + 2 * couples
+    is_paired = (z > middle) & (z < singles)
+    is_giver = is_paired & (lax.rem(z - middle, 2) == 1)
+    is_taker = is_paired & (lax.rem(z - middle, 2) == 0)
+    senders = middle + 1 + couples + nz - singles
+    slot = jnp.where(is_paired, middle + 1 + (z - middle - 1) // 2, jnp.where(z > middle, z - couples, z))
     rising = z <= nz // 2
     following = jnp.where(rising, z + FAN, z - FAN)
     preceding = jnp.where(rising, z - FAN, z + FAN)
@@ -114,11 +122,18 @@
         signal(barrier, spec=1 - s)
 
         def tell(i, carry):
-            signal(barrier, vel=i, spec=0)
-            signal(barrier, vel=i, spec=1)
+            @pl.when((i <= middle) | (i >= singles) | (lax.rem(i - middle, 2) == 0))
+            def _():
+                signal(barrier, vel=i, spec=0)
+                signal(barrier, vel=i, spec=1)
+
             return carry
 
         lax.fori_loop(1, nz, tell, 0)
+
+    @pl.when(is_taker)
+    def _():
+        signal(barrier, vel=z - 1)
 
     @pl.when(is_first)
     def _():
@@ -172,16 +187,30 @@
     def to_root():
         return pltpu.make_async_remote_copy(
             src_ref=msg,
-            dst_ref=inbox.at[z, s],
+            dst_ref=inbox.at[slot, s],
             send_sem=msg_send,
             recv_sem=inbox_sem.at[one(z > 0) + one(z > middle)],
             device_id={"vel": 0, "spec": ROOT},
             device_id_type=MESH,
         )
 
-    @pl.when(jnp.logical_not(is_root))
+    def to_taker():
+        return pltpu.make_async_remote_copy(
+            src_ref=msg,
+            dst_ref=relay,
+            send_sem=msg_send,
+            recv_sem=relay_sem,
+            device_id={"vel": z + 1},
+            device_id_type=MESH,
+        )
+
+    @pl.when(jnp.logical_not(is_root | is_paired))
     def _():
         to_root().start()
+
+    @pl.when(is_giver)
+    def _():
+        to_taker().start()
 
     def halo_copy(src, box, sends, recvs, side):
         return pltpu.make_async_remote_copy(
@@ -203,6 +232,12 @@
     @pl.when(is_member | is_handed)
     def _():
         signal(ready, vel=jnp.where(is_handed, preceding, leader))
+
+    @pl.when(is_taker)
+    def _():
+        settle(relay, relay_sem)
+        msg[...] += relay[...]
+        to_root().start()
 
     speed_unit = (STEP / root_m)[:, :1]
     ones = jnp.ones((8, vel), F32)
@@ -289,7 +324,7 @@
         ]
 
         own, other = mine, partner
-        for part, (low, high) in enumerate([(1, middle + 1), (middle + 1, nz)]):
+        for part, (low, high) in enumerate([(1, middle + 1), (middle + 1, senders)]):
             settle(inbox.at[pl.ds(low, high - low)], inbox_sem.at[part + 1])
             for i in range(low, high):
                 own += inbox[i, ROOT]
@@ -456,8 +491,9 @@
 
 def finish(coll, inner, lane, flux, out, edge, sem):
     slab = flux.shape[0]
+    for i in range(slab - 2):
+        pltpu.make_async_copy(inner.at[i], out.at[0, i + 1], sem.at[2]).start()
     copies = [pltpu.make_async_copy(inner, out.at[0, pl.ds(1, slab - 2)], sem.at[2])]
-    copies[0].start()
     for k, i in enumerate((0, slab - 1)):
         stream(coll, lane, flux, i, edge.at[k])
         copies.append(pltpu.make_async_copy(edge.at[k], out.at[0, i], sem.at[k]))
@@ -499,6 +535,7 @@
             pltpu.SMEM((2, slab), jnp.int32),
             pltpu.VMEM((ROWS, pairs, 128), F32),
             pltpu.VMEM((nz, 2, ROWS, pairs, 128), F32),
+            pltpu.VMEM((ROWS, pairs, 128), F32),
             pltpu.VMEM((pairs, 8, 128), F32),
             pltpu.VMEM((pairs, 8, 128), F32),
             pltpu.VMEM((2, cross, vel), F32),
@@ -508,6 +545,7 @@
             dma((4,)),
             dma(()),
             dma((3,)),
+            dma(()),
             dma((3,)),
             dma(()),
             dma((FAN,)),

time: 57.4 us -> 59.7 us (1.040)
  Pallas kernels: 56.6 us -> 58.9 us
    pallas_call x1, Pallas kernels: 55.3 us -> 57.5 us  [per_device(): pl.pallas_call(kernel, out_shape=passed, in_specs=[hbm] * 5, out_specs=[v...]
where the time goes in v6:
time: 59.7 us; the launch traced here: 59.5 us
  Pallas kernels  58.9 us (99%)
  between operations  0.66 us (1%)
    pallas_call x1, Pallas kernels, per_device(): pl.pallas_call(kernel, out_shape=passed, in_specs=[hbm] * 5, out_specs=[v...  57.5 us
    pallas_call x1, Pallas kernels, per_device(): pl.pallas_call(finish, out_shape=jax.ShapeDtypeStruct(distribution.shape,...  1.33 us

profile of v6, /device:TPU:33, one launch (start us, length us, event | category | flops | bytes accessed | tf_op | source)
XLA Modules:
  0.0 59.5 jit_solution(6916988398861872007)
XLA Ops:
  0.7 57.5 %shard_map.55 = (f32[10,64,1024]{2,1,0:T(8,128)S(1)}, f32[6,64,1024]{2,1,0:T(8,128)S(1)}, f32[8,1024]{1,0:T(8,128)S(1)}, f32[8,64,128]{2,1,0:T(8,128)S(1)}) custom-call(f32[1,8,64,1024]{3,2,1,0:T(8,128)} %dist_in.1, s32[1,1024]{1,0:T(1,128)} %bitcast.3, s32[1]{0:T(128)S(6)} %copy.6.mass_in, s32[2,8]{1,0:T(2,128)} %bitcast.4, s32[2,8]{1,0:T(2,128)} %bitcast.5), custom_call_target="tpu_custom_call" | custom-call | tf_op jit(solution)/shard_map/pallas_call | solution.py:525
  58.2 1.3 %shard_map.56 = f32[1,8,64,1024]{3,2,1,0:T(8,128)} custom-call(f32[10,64,1024]{2,1,0:T(8,128)S(1)} %get-tuple-element.9.coll, f32[6,64,1024]{2,1,0:T(8,128)S(1)} %get-tuple-element.10.inner, f32[8,1024]{1,0:T(8,128)S(1)} %get-tuple-element.11.lane, f32[8,64,128]{2,1,0:T(8,128)S(1)} %get-tuple-element.12.flux), custom_call_target="tpu_custom_call" | custom-call | tf_op jit(solution)/shard_map/pallas_call | solution.py:569

commit v7 on v5

--- a/solution.py
+++ b/solution.py
@@ -74,11 +74,9 @@
     is_leader = lax.rem(z, FAN) == 0
     leader = z - lax.rem(z, FAN)
     middle = nz // 2 - 1
-    rising = z <= nz // 2
-    following = jnp.where(rising, z + FAN, z - FAN)
-    preceding = jnp.where(rising, z - FAN, z + FAN)
+    following, preceding = z + FAN, z - FAN
     passes = is_leader & (z > 0)
-    hands_on = passes & jnp.where(rising, following <= nz // 2, following > nz // 2)
+    hands_on = passes & (z < nz - 2 * FAN)
     is_handed = passes & (z != FAN) & (z != nz - FAN)
     is_member = (z > FAN) & (leader != z)
     is_first = z < FAN
@@ -456,8 +454,9 @@
 
 def finish(coll, inner, lane, flux, out, edge, sem):
     slab = flux.shape[0]
+    for i in range(slab - 2):
+        pltpu.make_async_copy(inner.at[i], out.at[0, i + 1], sem.at[2]).start()
     copies = [pltpu.make_async_copy(inner, out.at[0, pl.ds(1, slab - 2)], sem.at[2])]
-    copies[0].start()
     for k, i in enumerate((0, slab - 1)):
         stream(coll, lane, flux, i, edge.at[k])
         copies.append(pltpu.make_async_copy(edge.at[k], out.at[0, i], sem.at[k]))

time: 57.4 us -> 56.4 us (0.983)
  Pallas kernels: 56.6 us -> 55.6 us
    pallas_call x1, Pallas kernels: 55.3 us -> 54.3 us  [per_device(): pl.pallas_call(kernel, out_shape=passed, in_specs=[hbm] * 5, out_specs=[v...]
where the time goes in v7:
time: 56.4 us; the launch traced here: 56.3 us
  Pallas kernels  55.6 us (99%)
  between operations  0.66 us (1%)
    pallas_call x1, Pallas kernels, per_device(): pl.pallas_call(kernel, out_shape=passed, in_specs=[hbm] * 5, out_specs=[v...  54.3 us
    pallas_call x1, Pallas kernels, per_device(): pl.pallas_call(finish, out_shape=jax.ShapeDtypeStruct(distribution.shape,...  1.33 us

profile of v7, /device:TPU:33, one launch (start us, length us, event | category | flops | bytes accessed | tf_op | source)
XLA Modules:
  0.0 56.3 jit_solution(9196555465379253243)
XLA Ops:
  0.7 54.3 %shard_map.55 = (f32[10,64,1024]{2,1,0:T(8,128)S(1)}, f32[6,64,1024]{2,1,0:T(8,128)S(1)}, f32[8,1024]{1,0:T(8,128)S(1)}, f32[8,64,128]{2,1,0:T(8,128)S(1)}) custom-call(f32[1,8,64,1024]{3,2,1,0:T(8,128)} %dist_in.1, s32[1,1024]{1,0:T(1,128)} %bitcast.3, s32[1]{0:T(128)S(6)} %copy.6.mass_in, s32[2,8]{1,0:T(2,128)} %bitcast.4, s32[2,8]{1,0:T(2,128)} %bitcast.5), custom_call_target="tpu_custom_call" | custom-call | tf_op jit(solution)/shard_map/pallas_call | solution.py:488
  55.0 1.3 %shard_map.56 = f32[1,8,64,1024]{3,2,1,0:T(8,128)} custom-call(f32[10,64,1024]{2,1,0:T(8,128)S(1)} %get-tuple-element.9.coll, f32[6,64,1024]{2,1,0:T(8,128)S(1)} %get-tuple-element.10.inner, f32[8,1024]{1,0:T(8,128)S(1)} %get-tuple-element.11.lane, f32[8,64,128]{2,1,0:T(8,128)S(1)} %get-tuple-element.12.flux), custom_call_target="tpu_custom_call" | custom-call | tf_op jit(solution)/shard_map/pallas_call | solution.py:530

commit v8 on v7

--- a/solution.py
+++ b/solution.py
@@ -172,7 +172,7 @@
             src_ref=msg,
             dst_ref=inbox.at[z, s],
             send_sem=msg_send,
-            recv_sem=inbox_sem.at[one(z > 0) + one(z > middle)],
+            recv_sem=inbox_sem.at[one(z > 0) + one(z > middle) + one(z >= nz - FAN)],
             device_id={"vel": 0, "spec": ROOT},
             device_id_type=MESH,
         )
@@ -232,7 +232,7 @@
 
     first, others, leaders = range(1, 2), range(2, FAN), sorted({FAN, nz - FAN})
 
-    def borders(places):
+    def borders(places, cores=(ROOT, 1 - ROOT)):
         return [
             pltpu.make_async_remote_copy(
                 src_ref=(coef if core == ROOT else coef_other).at[pairs - 1 if side == 0 else 0],
@@ -243,7 +243,7 @@
                 device_id_type=MESH,
             )
             for i in places
-            for core in (ROOT, 1 - ROOT)
+            for core in cores
             for side in range(2)
         ]
 
@@ -287,7 +287,7 @@
         ]
 
         own, other = mine, partner
-        for part, (low, high) in enumerate([(1, middle + 1), (middle + 1, nz)]):
+        for part, (low, high) in enumerate([(1, middle + 1), (middle + 1, nz - FAN), (nz - FAN, nz)]):
             settle(inbox.at[pl.ds(low, high - low)], inbox_sem.at[part + 1])
             for i in range(low, high):
                 own += inbox[i, ROOT]
@@ -323,9 +323,14 @@
             ]
             for i, values in enumerate(rows):
                 box[:, i, :] = values
+            if box is coef:
+                for copy in borders(range(1), (ROOT,)):
+                    copy.start()
 
         coef_copy(0, 1 - ROOT, False, coef_send.at[0]).start()
-        for copy in borders(range(1)) + served(first, coef_send.at[1]) + borders(first):
+        for copy in (
+            borders(range(1), (1 - ROOT,)) + served(first, coef_send.at[1]) + borders(first)
+        ):
             copy.start()
 
     @pl.when(jnp.logical_not(is_root))
@@ -506,7 +511,7 @@
             dma(()),
             dma((4,)),
             dma(()),
-            dma((3,)),
+            dma((4,)),
             dma((3,)),
             dma(()),
             dma((FAN,)),

time: 56.4 us -> 56.4 us (level)
  no operation moved by 1% of the time
where the time goes in v8:
time: 56.4 us; the launch traced here: 56.2 us
  Pallas kernels  55.6 us (99%)
  between operations  0.66 us (1%)
    pallas_call x1, Pallas kernels, per_device(): pl.pallas_call(kernel, out_shape=passed, in_specs=[hbm] * 5, out_specs=[v...  54.2 us
    pallas_call x1, Pallas kernels, per_device(): pl.pallas_call(finish, out_shape=jax.ShapeDtypeStruct(distribution.shape,...  1.33 us

profile of v8, /device:TPU:33, one launch (start us, length us, event | category | flops | bytes accessed | tf_op | source)
XLA Modules:
  0.0 56.2 jit_solution(2765119049286220537)
XLA Ops:
  0.7 54.2 %shard_map.55 = (f32[10,64,1024]{2,1,0:T(8,128)S(1)}, f32[6,64,1024]{2,1,0:T(8,128)S(1)}, f32[8,1024]{1,0:T(8,128)S(1)}, f32[8,64,128]{2,1,0:T(8,128)S(1)}) custom-call(f32[1,8,64,1024]{3,2,1,0:T(8,128)} %dist_in.1, s32[1,1024]{1,0:T(1,128)} %bitcast.3, s32[1]{0:T(128)S(6)} %copy.6.mass_in, s32[2,8]{1,0:T(2,128)} %bitcast.4, s32[2,8]{1,0:T(2,128)} %bitcast.5), custom_call_target="tpu_custom_call" | custom-call | tf_op jit(solution)/shard_map/pallas_call | solution.py:493
  54.9 1.3 %shard_map.56 = f32[1,8,64,1024]{3,2,1,0:T(8,128)} custom-call(f32[10,64,1024]{2,1,0:T(8,128)S(1)} %get-tuple-element.9.coll, f32[6,64,1024]{2,1,0:T(8,128)S(1)} %get-tuple-element.10.inner, f32[8,1024]{1,0:T(8,128)S(1)} %get-tuple-element.11.lane, f32[8,64,128]{2,1,0:T(8,128)S(1)} %get-tuple-element.12.flux), custom_call_target="tpu_custom_call" | custom-call | tf_op jit(solution)/shard_map/pallas_call | solution.py:535
